TPU v7x, 256 devices: a whole 4x4x8 slice. The times are simulated.
256 devices in a mesh: dom: 64 (over z, x, core), rep: 4 (over y).
Axes of the slice: x: 4, y: 4, z: 8, core: 2. Of those that a mesh axis runs over, the one named last changes fastest.
Arguments:
- features: bfloat16 [524288, 128], P('dom'), may hold values from -6 to 6
- weight: bfloat16 [128, 256], replicated, may hold values from -0.5 to 0.5
- out_grad: bfloat16 [524288, 256], P(('dom', 'rep')), may hold values from -6 to 6
- send_rows: int32 [64, 64, 64], P('dom'), may hold values from 0 to 8191, as said below
- send_count: int32 [64, 64], P('dom'), may hold values from 0 to 64, as said below
- tile_target: int32 [64, 4, 256], P('dom', 'rep'), may hold values from 0 to 15, as said below
- tile_source: int32 [64, 4, 256], P('dom', 'rep'), may hold values from 0 to 95, as said below
- tile_weights: bfloat16 [64, 4, 256, 128, 128], P('dom', 'rep'), may hold values from -0.125 to 0.125
Outputs:
- activated: bfloat16 [524288, 256], P(('dom', 'rep'))
- feature_grad: bfloat16 [524288, 128], P(('dom', 'rep'))
- weight_grad: float32 [128, 256], replicated
Inputs may be any that keep to these rules, and one draw needn't show every extreme that they name: Within one list send_rows[o, d] the rows are distinct and increasing; entries at slots c >= send_count[o, d] are ignored. send_count[o, o] is 0. Every owner sends exactly 64 rows to some partition, and every partition receives exactly 64 rows from some owner. `tile_target`: pairs of target and source tiles may repeat. `tile_source`: every halo source tile (64 to 95) is named by some tile of every group.
All inputs are finite; a program needn't handle non-finite values.
Results may differ from a plain program's by a relative error of at most 0.006.
Values may be sent and summed in bfloat16 or wider, within the bound.
A program may use at most 128 MiB of HBM per device.

v0:
```python
import jax
import jax.numpy as jnp
from jax import lax
from jax.sharding import Mesh
from jax.sharding import PartitionSpec as P

DOM = ("dom_0", "dom_1", "dom_2")
DOM_REP = ("dom_0", "dom_1", "dom_2", "rep")


def split_up(shard, dim, devices):
    before, after = (shard.shape[:dim], shard.shape[dim + 1 :])
    return jnp.moveaxis(shard.reshape(*before, devices, -1, *after), dim, 0)


def sent_and_summed(shard, axis, dim):
    pieces = split_up(shard, dim, lax.axis_size(axis))
    arrived = lax.all_to_all(pieces, axis, split_axis=0, concat_axis=0, tiled=True)
    return arrived.sum(axis=0)


def sum_by_axis(shard, axes, dim):
    far, near = axes
    pieces = split_up(shard, dim, lax.axis_size(far))
    nearer = sent_and_summed(pieces, near, dim + 1)
    arrived = lax.all_to_all(nearer, far, split_axis=0, concat_axis=0, tiled=True)
    return arrived.sum(axis=0)


def filled_up(lines, devices):
    spare = -len(lines) % devices
    return jnp.pad(lines, [(0, spare)] + [(0, 0)] * (lines.ndim - 1))


def from_everyone(shard, axis):
    copies = jnp.broadcast_to(shard, (lax.axis_size(axis), *shard.shape))
    return lax.all_to_all(copies, axis, split_axis=0, concat_axis=0, tiled=True)


def in_order(pieces, dim):
    pieces = jnp.moveaxis(pieces, 0, dim)
    shape = pieces.shape
    return pieces.reshape(*shape[:dim], shape[dim] * shape[dim + 1], *shape[dim + 2 :])


def gather_axes(shard, axes, dim):
    far, near = axes
    leading = from_everyone(shard, far)
    pieces = jnp.swapaxes(from_everyone(leading, near), 0, 1)
    return in_order(pieces.reshape(-1, *shard.shape), dim)


def nested_sum(shard, axes):
    lines = shard.reshape(-1)
    own = sum_by_axis(filled_up(lines, lax.axis_size(axes[0]) * lax.axis_size(axes[1])), axes, 0)
    whole = gather_axes(own, axes, 0)
    return whole[: len(lines)].reshape(shard.shape)


def shards(
    features, weight, out_grad, send_rows, send_count, tile_target, tile_source, tile_weights
):
    feat = features.shape[1]
    tile = tile_weights.shape[-1]
    rows = send_rows[0]
    counts = send_count[0]
    width = rows.shape[1]
    valid = jnp.arange(width, dtype=jnp.int32)[None, :] < counts[:, None]
    outgoing = jnp.where(valid[:, :, None], features[rows], jnp.zeros((), jnp.bfloat16))
    halo = lax.all_to_all(outgoing, DOM, split_axis=0, concat_axis=0, tiled=True)
    sources = jnp.concatenate([features, halo.reshape(-1, feat)], axis=0)
    targets = tile_target[0, 0]
    anchors = tile_source[0, 0]
    values = tile_weights[0, 0]
    tgt_count = out_grad.shape[0] // tile
    src_count = sources.shape[0] // tile
    blocks = sources.reshape(src_count, tile, feat)[anchors]
    prods = jnp.einsum("tij,tjf->tif", values, blocks, preferred_element_type=jnp.float32)
    gathered = jax.ops.segment_sum(prods, targets, num_segments=tgt_count)
    gathered = gathered.reshape(-1, feat).astype(jnp.bfloat16)
    pre = jnp.dot(gathered, weight, preferred_element_type=jnp.float32)
    activated = jax.nn.silu(pre).astype(jnp.bfloat16)
    sigma = jax.nn.sigmoid(pre)
    slope = sigma * (1.0 + pre * (1.0 - sigma))
    pre_grad = (out_grad.astype(jnp.float32) * slope).astype(jnp.bfloat16)
    weight_part = jnp.dot(gathered.T, pre_grad, preferred_element_type=jnp.float32)
    weight_grad = nested_sum(weight_part, (("dom_0", "dom_1"), ("dom_2", "rep")))
    agg_grad = jnp.dot(pre_grad, weight.T, preferred_element_type=jnp.float32).astype(jnp.bfloat16)
    dblocks = agg_grad.reshape(tgt_count, tile, feat)[targets]
    backward = jnp.einsum("tij,tif->tjf", values, dblocks, preferred_element_type=jnp.float32)
    source_grad = jax.ops.segment_sum(backward, anchors, num_segments=src_count).reshape(-1, feat)
    owned_rows = features.shape[0]
    local = source_grad[:owned_rows]
    incoming = source_grad[owned_rows:].reshape(-1, width, feat)
    returned = lax.all_to_all(incoming, DOM, split_axis=0, concat_axis=0, tiled=True)
    kept = jnp.where(valid[:, :, None], returned, jnp.zeros((), jnp.float32))
    local = local.at[rows.reshape(-1)].add(kept.reshape(-1, feat))
    node_grad = sent_and_summed(local, "rep", 0).astype(jnp.bfloat16)
    return (activated, node_grad, weight_grad)


def solution(mesh):
    finer = Mesh(
        mesh.devices.reshape(8, 4, 2, mesh.shape["rep"]), ("dom_0", "dom_1", "dom_2", "rep")
    )
    in_specs = (
        P(DOM, None),
        P(),
        P(DOM_REP, None),
        P(DOM, None, None),
        P(DOM, None),
        P(DOM, "rep", None),
        P(DOM, "rep", None),
        P(DOM, "rep", None, None, None),
    )
    out_specs = (P(DOM_REP, None), P(DOM_REP, None), P())
    return jax.shard_map(
        shards, mesh=finer, in_specs=in_specs, out_specs=out_specs, check_vma=False
    )
```

profile of v0, /device:TPU:1, one launch (start us, length us, event | category | flops | bytes accessed | tf_op | source)
XLA Modules:
  0.0 422.0 jit_solution(2858136513586759027)
XLA Ops:
  0.6 0.8 iota_compare_fusion
  1.4 0.8 compare_select_fusion.1
  2.3 13.0 %gather_fusion = bf16[4096,128]{1,0:T(8,128)(2,1)S(1)} fusion(bf16[8192,128]{1,0:T(8,128)(2,1)} %param.8, s32[4096]{0:T(1024)S(1)} %broadcast_clamp_fusion), kind=kCustom, calls=%fused_computation | custom fusion | bytes 2113536 | tf_op jit(solution)/shard_map/gather | solution.py:69
  15.3 1.5 broadcast_select_fusion.1
  16.8 13.0 %all-to-all-start = ((bf16[64,64,128]{2,1,0:T(8,128)(2,1)}), bf16[64,64,128]{2,1,0:T(8,128)(2,1)S(1)}, u32[]{:S(2)}, u32[]{:S(2)}) async-start(bf16[64,64,128]{2,1,0:T(8,128)(2,1)} %broadcast_select_fusion.1), calls=%async_computation | async-start | bytes 2097152 | tf_op jit(solution)/shard_map/all_to_all | solution.py:70
  29.8 28.1 %all-to-all-done = bf16[64,64,128]{2,1,0:T(8,128)(2,1)S(1)} async-done(((bf16[64,64,128]{2,1,0:T(8,128)(2,1)}), bf16[64,64,128]{2,1,0:T(8,128)(2,1)S(1)}, u32[]{:S(2)}, u32[]{:S(2)}) %all-to-all-start) | async-done | bytes 1048608 | tf_op jit(solution)/shard_map/all_to_all | solution.py:70
  58.0 10.3 %pad_maximum_fusion = bf16[12288,128]{1,0:T(8,128)(2,1)} fusion(bf16[4096,128]{1,0:T(8,128)(2,1)S(1)} %bitcast.53, bf16[8192,128]{1,0:T(8,128)(2,1)S(1)} %copy-done.2), kind=kLoop, calls=%fused_computation.10 | loop fusion | flops 6291456 | bytes 6291456 | tf_op jit(solution)/shard_map/concatenate | solution.py:71
  68.3 10.5 %gather_fusion.1 = bf16[256,128,128]{2,1,0:T(8,128)(2,1)} fusion(bf16[96,128,128]{2,1,0:T(8,128)(2,1)} %bitcast.49, s32[1024]{0:T(1024)S(1)} %pad_clamp_fusion.1), kind=kCustom, calls=%fused_computation.1 | custom fusion | bytes 16778240 | tf_op jit(solution)/shard_map/gather | solution.py:77
  78.8 12.8 %convolution_bitcast_fusion.1 = f32[256,128,128]{1,2,0:T(8,128)} fusion(bf16[256,128,128]{2,1,0:T(8,128)(2,1)} %gather_fusion.1, bf16[1,1,256,128,128]{4,3,2,1,0:T(8,128)(2,1)} %param.15), kind=kOutput, calls=%fused_computation.7 | convolution fusion | flops 1073741824 | bytes 33554432 | tf_op jit(solution)/shard_map/tij,tjf->tif/dot_general | solution.py:78
  91.7 17.5 %copy.23 = f32[256,128,128]{2,1,0:T(8,128)} copy(f32[256,128,128]{1,2,0:T(8,128)} %convolution_bitcast_fusion.1) | data formatting | bytes 33554432 | tf_op jit(solution)/shard_map/tij,tjf->tif/dot_general | solution.py:78
  109.2 33.3 %scatter_fusion = f32[16,128,128]{2,1,0:T(8,128)S(1)} fusion(f32[16,128,128]{2,1,0:T(8,128)S(1)} %broadcast_in_dim.41, s32[256]{0:T(256)S(1)} %bitcast.59, f32[256,128,128]{2,1,0:T(8,128)} %copy.23), kind=kCustom, calls=%fused_computation.3 | custom fusion | flops 4194304 | bytes 50332672 | tf_op jit(solution)/shard_map/scatter-add | solution.py:79
  142.7 2.1 multiply_convert_fusion
  145.9 5.6 %all-to-all-start.3 = ((f32[8,32,128]{2,1,0:T(8,128)}), f32[8,32,128]{2,1,0:T(8,128)S(1)}, u32[]{:S(2)}, u32[]{:S(2)}) async-start(f32[8,32,128]{2,1,0:T(8,128)} %bitcast.45), calls=%async_computation.3 | async-start | bytes 262144 | tf_op jit(solution)/shard_map/all_to_all | solution.py:18
  151.5 5.2 %all-to-all-done.3 = f32[8,32,128]{2,1,0:T(8,128)S(1)} async-done(((f32[8,32,128]{2,1,0:T(8,128)}), f32[8,32,128]{2,1,0:T(8,128)S(1)}, u32[]{:S(2)}, u32[]{:S(2)}) %all-to-all-start.3) | async-done | bytes 131104 | tf_op jit(solution)/shard_map/all_to_all | solution.py:18
  157.3 4.7 %all-to-all-start.4 = ((f32[32,1,128]{2,1,0:T(1,128)}), f32[32,1,128]{2,1,0:T(1,128)S(1)}, u32[]{:S(2)}, u32[]{:S(2)}) async-start(f32[32,1,128]{2,1,0:T(1,128)} %bitcast.22), calls=%async_computation.4 | async-start | bytes 32768 | tf_op jit(solution)/shard_map/all_to_all | solution.py:26
  162.4 8.6 %gather_fusion.2 = bf16[256,128,128]{2,1,0:T(8,128)(2,1)} fusion(bf16[16,128,128]{2,1,0:T(8,128)(2,1)S(1)} %bitcast.46, s32[1024]{0:T(1024)S(1)} %pad_clamp_fusion), kind=kCustom, calls=%fused_computation.2 | custom fusion | bytes 16778240 | tf_op jit(solution)/shard_map/gather | solution.py:89
  171.7 9.2 %all-to-all-start.5 = ((f32[32,1,128]{2,1,0:T(1,128)}), f32[32,1,128]{2,1,0:T(1,128)S(1)}, u32[]{:S(2)}, u32[]{:S(2)}) async-start(f32[32,1,128]{2,1,0:T(1,128)} %broadcast_in_dim.46), calls=%async_computation.5 | async-start | bytes 32768 | tf_op jit(solution)/shard_map/all_to_all | solution.py:37
  180.9 14.4 %convolution_bitcast_fusion = f32[256,128,128]{1,2,0:T(8,128)} fusion(bf16[256,128,128]{2,1,0:T(8,128)(2,1)} %gather_fusion.2, bf16[1,1,256,128,128]{4,3,2,1,0:T(8,128)(2,1)} %param.15), kind=kOutput, calls=%fused_computation.6 | convolution fusion | flops 1073741824 | bytes 33554432 | tf_op jit(solution)/shard_map/tij,tif->tjf/dot_general | solution.py:90
  195.3 17.4 %copy.25 = f32[256,128,128]{2,1,0:T(8,128)} copy(f32[256,128,128]{1,2,0:T(8,128)} %convolution_bitcast_fusion) | data formatting | bytes 33554432 | tf_op jit(solution)/shard_map/tij,tif->tjf/dot_general | solution.py:90
  212.7 3.4 broadcast_in_dim.44
  216.1 51.8 %scatter_fusion.1 = f32[96,128,128]{2,1,0:T(8,128)} fusion(f32[96,128,128]{2,1,0:T(8,128)} %broadcast_in_dim.44, s32[256]{0:T(256)S(1)} %bitcast.60, f32[256,128,128]{2,1,0:T(8,128)} %copy.25), kind=kCustom, calls=%fused_computation.4 | custom fusion | flops 4194304 | bytes 50332672 | tf_op jit(solution)/shard_map/scatter-add | solution.py:91
  267.9 3.1 slice.20
  271.1 11.3 %all-to-all-start.1 = ((f32[64,64,128]{2,1,0:T(8,128)}), f32[64,64,128]{2,1,0:T(8,128)S(1)}, u32[]{:S(2)}, u32[]{:S(2)}) async-start(f32[64,64,128]{2,1,0:T(8,128)} %bitcast.51), calls=%async_computation.1 | async-start | bytes 4194304 | tf_op jit(solution)/shard_map/all_to_all | solution.py:95
  282.5 4.6 %slice.19 = f32[64,128,128]{2,1,0:T(8,128)} slice(f32[96,128,128]{2,1,0:T(8,128)} %scatter_fusion.1), slice={[0:64], [0:128], [0:128]} | slice | bytes 8388608 | tf_op jit(solution)/shard_map/slice | solution.py:93
  287.1 45.0 %all-to-all-done.1 = f32[64,64,128]{2,1,0:T(8,128)S(1)} async-done(((f32[64,64,128]{2,1,0:T(8,128)}), f32[64,64,128]{2,1,0:T(8,128)S(1)}, u32[]{:S(2)}, u32[]{:S(2)}) %all-to-all-start.1) | async-done | bytes 2097184 | tf_op jit(solution)/shard_map/all_to_all | solution.py:95
  332.1 0.7 broadcast_in_dim.47
  333.4 5.4 %all-to-all-start.6 = ((f32[8,32,128]{2,1,0:T(8,128)}), f32[8,32,128]{2,1,0:T(8,128)S(1)}, u32[]{:S(2)}, u32[]{:S(2)}) async-start(f32[8,32,128]{2,1,0:T(8,128)} %broadcast_in_dim.47), calls=%async_computation.6 | async-start | bytes 262144 | tf_op jit(solution)/shard_map/all_to_all | solution.py:37
  338.8 1.9 broadcast_select_fusion
  340.8 24.2 %scatter_fusion.2 = f32[8192,128]{1,0:T(8,128)} fusion(f32[8192,128]{1,0:T(8,128)} %bitcast.47, s32[4096]{0:T(1024)S(1)} %bitcast.57, f32[4096,128]{1,0:T(8,128)S(1)} %bitcast.50), kind=kCustom, calls=%fused_computation.5 | custom fusion | flops 524288 | bytes 6307840 | tf_op jit(solution)/shard_map/scatter-add | solution.py:97
  365.0 5.0 %all-to-all-start.2 = ((f32[4,2048,128]{2,1,0:T(8,128)}), f32[4,2048,128]{2,1,0:T(8,128)}, u32[]{:S(2)}, u32[]{:S(2)}) async-start(f32[4,2048,128]{2,1,0:T(8,128)} %bitcast.48), calls=%async_computation.2 | async-start | bytes 8388608 | tf_op jit(solution)/shard_map/all_to_all | solution.py:18
  370.7 47.9 %all-to-all-done.2 = f32[4,2048,128]{2,1,0:T(8,128)} async-done(((f32[4,2048,128]{2,1,0:T(8,128)}), f32[4,2048,128]{2,1,0:T(8,128)}, u32[]{:S(2)}, u32[]{:S(2)}) %all-to-all-start.2) | async-done | bytes 4194336 | tf_op jit(solution)/shard_map/all_to_all | solution.py:18
  418.6 3.4 reduce_sum.27
  (38 shorter events, 4.6 us)
Async XLA Ops:
  0.6 142.1 %copy-start = (bf16[128,256]{1,0:T(8,128)(2,1)S(1)}, bf16[128,256]{1,0:T(8,128)(2,1)}, u32[]{:S(2)}) copy-start(bf16[128,256]{1,0:T(8,128)(2,1)} %param.9) | copy-start | bytes 196612
  2.3 27.5 %copy-start.6 = (s32[1,1,256]{2,1,0:T(1,128)S(1)}, s32[1,1,256]{2,1,0:T(1,128)}, u32[]{:S(2)}) copy-start(s32[1,1,256]{2,1,0:T(1,128)} %param.14) | copy-start | bytes 3076
  2.3 55.7 %copy-start.2 = (bf16[8192,128]{1,0:T(8,128)(2,1)S(1)}, bf16[8192,128]{1,0:T(8,128)(2,1)}, u32[]{:S(2)}) copy-start(bf16[8192,128]{1,0:T(8,128)(2,1)} %param.8) | copy-start | bytes 6291460
  16.8 41.1 %all-to-all-start = ((bf16[64,64,128]{2,1,0:T(8,128)(2,1)}), bf16[64,64,128]{2,1,0:T(8,128)(2,1)S(1)}, u32[]{:S(2)}, u32[]{:S(2)}) async-start(bf16[64,64,128]{2,1,0:T(8,128)(2,1)} %broadcast_select_fusion.1), calls=%async_computation | async-start | bytes 2097152 | tf_op jit(solution)/shard_map/all_to_all | solution.py:70
  91.7 17.6 %copy-start.5 = (s32[1,1,256]{2,1,0:T(1,128)S(1)}, s32[1,1,256]{2,1,0:T(1,128)}, u32[]{:S(2)}) copy-start(s32[1,1,256]{2,1,0:T(1,128)} %param.13) | copy-start | bytes 3076
  109.2 33.5 %copy-start.7 = (bf16[2048,256]{1,0:T(8,128)(2,1)S(1)}, bf16[2048,256]{1,0:T(8,128)(2,1)}, u32[]{:S(2)}) copy-start(bf16[2048,256]{1,0:T(8,128)(2,1)} %param.10) | copy-start | bytes 3145732
  145.9 10.8 %all-to-all-start.3 = ((f32[8,32,128]{2,1,0:T(8,128)}), f32[8,32,128]{2,1,0:T(8,128)S(1)}, u32[]{:S(2)}, u32[]{:S(2)}) async-start(f32[8,32,128]{2,1,0:T(8,128)} %bitcast.45), calls=%async_computation.3 | async-start | bytes 262144 | tf_op jit(solution)/shard_map/all_to_all | solution.py:18
  157.3 13.7 %all-to-all-start.4 = ((f32[32,1,128]{2,1,0:T(1,128)}), f32[32,1,128]{2,1,0:T(1,128)S(1)}, u32[]{:S(2)}, u32[]{:S(2)}) async-start(f32[32,1,128]{2,1,0:T(1,128)} %bitcast.22), calls=%async_computation.4 | async-start | bytes 32768 | tf_op jit(solution)/shard_map/all_to_all | solution.py:26
  171.7 99.4 %all-to-all-start.5 = ((f32[32,1,128]{2,1,0:T(1,128)}), f32[32,1,128]{2,1,0:T(1,128)S(1)}, u32[]{:S(2)}, u32[]{:S(2)}) async-start(f32[32,1,128]{2,1,0:T(1,128)} %broadcast_in_dim.46), calls=%async_computation.5 | async-start | bytes 32768 | tf_op jit(solution)/shard_map/all_to_all | solution.py:37
  267.9 14.5 %copy-start.4 = (s32[1,64,64]{2,1,0:T(8,128)S(1)}, s32[1,64,64]{2,1,0:T(8,128)}, u32[]{:S(2)}) copy-start(s32[1,64,64]{2,1,0:T(8,128)} %param.11) | copy-start | bytes 49156
  271.1 61.0 %all-to-all-start.1 = ((f32[64,64,128]{2,1,0:T(8,128)}), f32[64,64,128]{2,1,0:T(8,128)S(1)}, u32[]{:S(2)}, u32[]{:S(2)}) async-start(f32[64,64,128]{2,1,0:T(8,128)} %bitcast.51), calls=%async_computation.1 | async-start | bytes 4194304 | tf_op jit(solution)/shard_map/all_to_all | solution.py:95
  332.1 1.4 copy-start.3
  333.4 31.5 %all-to-all-start.6 = ((f32[8,32,128]{2,1,0:T(8,128)}), f32[8,32,128]{2,1,0:T(8,128)S(1)}, u32[]{:S(2)}, u32[]{:S(2)}) async-start(f32[8,32,128]{2,1,0:T(8,128)} %broadcast_in_dim.47), calls=%async_computation.6 | async-start | bytes 262144 | tf_op jit(solution)/shard_map/all_to_all | solution.py:37
  365.0 57.0 %copy-start.1 = (bf16[128,256]{1,0:T(8,128)(2,1)S(1)}, bf16[128,256]{1,0:T(8,128)(2,1)}, u32[]{:S(2)}) copy-start(bf16[128,256]{1,0:T(8,128)(2,1)} %param.9) | copy-start | bytes 196612
  365.0 53.6 %all-to-all-start.2 = ((f32[4,2048,128]{2,1,0:T(8,128)}), f32[4,2048,128]{2,1,0:T(8,128)}, u32[]{:S(2)}, u32[]{:S(2)}) async-start(f32[4,2048,128]{2,1,0:T(8,128)} %bitcast.48), calls=%async_computation.2 | async-start | bytes 8388608 | tf_op jit(solution)/shard_map/all_to_all | solution.py:18
where the time goes:
time: 425 us; the launch traced here: 422 us
  other arithmetic  129 us (30%)
  waiting for transfers between devices  126 us (30%)
  local copies, waits for them, and re-layouts  82 us (19%)
  starting transfers between devices  54.1 us (13%)
  matrix products  30.1 us (7%)
    all_to_all x2, waiting for transfers between devices, sent_and_summed(): lax.all_to_all(pieces, axis, split_axis=0, concat_axis=0, tiled=True)  53 us
    scatter-add x1, other arithmetic, shards(): jax.ops.segment_sum(backward, anchors, num_segments=src_count)  51.8 us
    all_to_all x1, waiting for transfers between devices, shards(): lax.all_to_all(incoming, DOM, split_axis=0, concat_axis=0, tiled=True)  45 us
    scatter-add x1, other arithmetic, shards(): gathered = jax.ops.segment_sum(prods, targets, num_segments=tgt_count)  33.3 us
    all_to_all x1, waiting for transfers between devices, shards(): lax.all_to_all(outgoing, DOM, split_axis=0, concat_axis=0, tiled=True)  28.1 us
    scatter-add x1, other arithmetic, shards(): local = local.at[rows.reshape(-1)].add(kept.reshape(-1, feat))  24.2 us
    dot_general x1, local copies, waits for them, and re-layouts, shards(): jnp.einsum('tij,tjf->tif', values, blocks, preferred_element_type=jnp.flo...  17.5 us
    dot_general x1, local copies, waits for them, and re-layouts, shards(): jnp.einsum('tij,tif->tjf', values, dblocks, preferred_element_type=jnp.fl...  17.4 us
  transfers between devices with their start and end apart: 7, of which 4 were waited for; matrix products, arithmetic and copies ran while one was open for 31% of the time, Pallas kernels for 0%

commit v1 on v0

v1 whole, which is shorter than its diff:
```python
import functools

import jax
import jax.numpy as jnp
from jax import lax
from jax.experimental import pallas as pl
from jax.experimental.pallas import tpu as pltpu
from jax.sharding import PartitionSpec as P

F32 = jnp.float32
BF16 = jnp.bfloat16
TILE = 128
FEAT = 128
HID = 256
CAP = 64
NDOM = 64
NREP = 4
Q = CAP // NREP
ROWS = 8192
TGT = 16
NT = 256
SRC = 96
LOCAL = 64
CHUNKS = 16
PER = NT // CHUNKS

VMEM = pl.BlockSpec(memory_space=pltpu.VMEM)
SMEM = pl.BlockSpec(memory_space=pltpu.SMEM)
ANY = pl.BlockSpec(memory_space=pl.ANY)
MESH = pl.DeviceIdType.MESH


def peer_id(d, r):
    return (d, r)


def gather_kernel(rows, counts, feats, out, wide, picked):
    rep = lax.axis_index("rep")
    wide[pl.ds(0, ROWS), :] = feats[...].astype(F32)
    wide[pl.ds(ROWS, 8), :] = jnp.zeros((8, FEAT), F32)

    @pl.loop(0, NDOM)
    def _(d):
        live = counts[0, d]
        for c in range(Q):
            slot = rep * Q + c
            row = jnp.where(slot < live, rows[0, d, slot], ROWS)
            picked[pl.ds(d * Q + c, 1), :] = wide[pl.ds(row, 1), :]

    out[...] = picked[...].reshape(NDOM, Q, FEAT).astype(BF16)


def gather_rows(rows, counts, feats):
    return pl.pallas_call(
        gather_kernel,
        out_shape=jax.ShapeDtypeStruct((NDOM, Q, FEAT), BF16),
        in_specs=[SMEM, SMEM, VMEM],
        out_specs=VMEM,
        scratch_shapes=[
            pltpu.VMEM((ROWS + 8, FEAT), F32),
            pltpu.VMEM((NDOM * Q, FEAT), F32),
        ],
        name="gather_rows",
    )(rows, counts, feats)


def greet_all(me_d, me_r):
    barrier = pltpu.get_barrier_semaphore()

    @pl.loop(1, NDOM)
    def _(k):
        pl.semaphore_signal(
            barrier, inc=1, device_id=peer_id(lax.rem(me_d + k, NDOM), me_r), device_id_type=MESH
        )

    for k in range(1, NREP):
        pl.semaphore_signal(
            barrier, inc=1, device_id=peer_id(me_d, lax.rem(me_r + k, NREP)), device_id_type=MESH
        )
    pl.semaphore_wait(barrier, NDOM - 1 + NREP - 1)


def halo_kernel(send, halo, own_sem, send_sem, recv_sem, share_send, share_recv):
    me_d = lax.axis_index("dom")
    me_r = lax.axis_index("rep")
    greet_all(me_d, me_r)

    def to(k):
        d = lax.rem(me_d + k, NDOM)
        return pltpu.make_async_remote_copy(
            src_ref=send.at[d],
            dst_ref=halo.at[me_d, me_r],
            send_sem=send_sem.at[k],
            recv_sem=recv_sem.at[k],
            device_id=peer_id(d, me_r),
            device_id_type=MESH,
        )

    def came(k):
        d = lax.rem(me_d + NDOM - k, NDOM)
        return pltpu.make_async_remote_copy(
            src_ref=send.at[d],
            dst_ref=halo.at[d, me_r],
            send_sem=send_sem.at[k],
            recv_sem=recv_sem.at[k],
            device_id=peer_id(d, me_r),
            device_id_type=MESH,
        )

    own = pltpu.make_async_copy(send.at[me_d], halo.at[me_d, me_r], own_sem)
    own.start()

    @pl.loop(1, NDOM)
    def _(k):
        to(k).start()

    own.wait()

    @pl.loop(1, NDOM)
    def _(k):
        came(k).wait_recv()

    shares = []
    for k in range(1, NREP):
        share = pltpu.make_async_remote_copy(
            src_ref=halo.at[:, me_r],
            dst_ref=halo.at[:, me_r],
            send_sem=share_send.at[k],
            recv_sem=share_recv.at[k],
            device_id=peer_id(me_d, lax.rem(me_r + k, NREP)),
            device_id_type=MESH,
        )
        share.start()
        shares.append(share)

    @pl.loop(1, NDOM)
    def _(k):
        to(k).wait_send()

    for k in range(1, NREP):
        r = lax.rem(me_r + NREP - k, NREP)
        pltpu.make_async_remote_copy(
            src_ref=halo.at[:, r],
            dst_ref=halo.at[:, r],
            send_sem=share_send.at[k],
            recv_sem=share_recv.at[k],
            device_id=peer_id(me_d, r),
            device_id_type=MESH,
        ).wait_recv()
    for share in shares:
        share.wait_send()


def exchange_halo(send):
    return pl.pallas_call(
        halo_kernel,
        out_shape=jax.ShapeDtypeStruct((NDOM, NREP, Q, FEAT), BF16),
        in_specs=[VMEM],
        out_specs=VMEM,
        scratch_shapes=[
            pltpu.SemaphoreType.DMA,
            pltpu.SemaphoreType.DMA((NDOM,)),
            pltpu.SemaphoreType.DMA((NDOM,)),
            pltpu.SemaphoreType.DMA((NREP,)),
            pltpu.SemaphoreType.DMA((NREP,)),
        ],
        compiler_params=pltpu.CompilerParams(collective_id=0, has_side_effects=True),
        name="exchange_halo",
    )(send)


def layer_kernel(
    targets, anchors, feats, halo, tiles, grads, weight,
    act_out, local_out, halo_out, wgrad_out,
    src, wt, og, agg, gt, sg, act, sgb, wg,
    src_sem, wt_sem, og_sem, out_sem,
):
    loads = [
        pltpu.make_async_copy(feats, src.at[pl.ds(0, LOCAL)], src_sem.at[0]),
        pltpu.make_async_copy(halo, src.at[pl.ds(LOCAL, SRC - LOCAL)], src_sem.at[1]),
    ]
    for load in loads:
        load.start()

    def tile_load(c):
        part = pl.ds(c * PER, PER)
        return pltpu.make_async_copy(tiles.at[part], wt.at[part], wt_sem.at[c])

    for c in range(CHUNKS):
        tile_load(c).start()
    grad_load = pltpu.make_async_copy(grads, og, og_sem)
    grad_load.start()

    agg[...] = jnp.zeros_like(agg)
    sg[...] = jnp.zeros_like(sg)
    wg[...] = jnp.zeros_like(wg)
    for load in loads:
        load.wait()

    @pl.loop(0, CHUNKS)
    def _(c):
        tile_load(c).wait()
        for u in range(PER):
            t = c * PER + u
            prod = jnp.dot(wt[t], src[anchors[0, 0, t]], preferred_element_type=F32)
            k = targets[0, 0, t]
            agg[k] = agg[k] + prod

    grad_load.wait()

    @pl.loop(0, TGT)
    def _(k):
        gathered = agg[k].astype(BF16)
        pre = jnp.dot(gathered, weight[...], preferred_element_type=F32)
        sigma = jax.nn.sigmoid(pre)
        part = pl.ds(pl.multiple_of(k * TILE, TILE), TILE)
        act[part, :] = (pre * sigma).astype(BF16)
        slope = sigma * (1.0 + pre * (1.0 - sigma))
        pre_grad = (og[part, :].astype(F32) * slope).astype(BF16)
        wg[...] += lax.dot_general(
            gathered, pre_grad, (((0,), (0,)), ((), ())), preferred_element_type=F32
        )
        gt[k] = lax.dot_general(
            weight[...], pre_grad, (((1,), (1,)), ((), ())), preferred_element_type=F32
        ).astype(BF16)

    act_save = pltpu.make_async_copy(act, act_out, out_sem.at[0])
    act_save.start()
    wgrad_out[...] = jnp.concatenate([wg[:, :TILE], wg[:, TILE:]], axis=0)

    @pl.loop(0, CHUNKS)
    def _(c):
        for u in range(PER):
            t = c * PER + u
            prod = jnp.dot(gt[targets[0, 0, t]], wt[t], preferred_element_type=F32)
            s = anchors[0, 0, t]
            sg[s] = sg[s] + prod

    one = (
        lax.broadcasted_iota(jnp.int32, (TILE, TILE), 0)
        == lax.broadcasted_iota(jnp.int32, (TILE, TILE), 1)
    ).astype(F32).astype(BF16)

    @pl.loop(0, SRC // 8)
    def _(c):
        for u in range(8):
            s = c * 8 + u
            sgb[s] = lax.dot_general(
                one, sg[s].astype(BF16), (((1,), (1,)), ((), ())), preferred_element_type=F32
            ).astype(BF16)

    saves = [
        pltpu.make_async_copy(sgb.at[pl.ds(0, LOCAL)], local_out, out_sem.at[1]),
        pltpu.make_async_copy(sgb.at[pl.ds(LOCAL, SRC - LOCAL)], halo_out, out_sem.at[2]),
    ]
    for save in saves:
        save.start()
    act_save.wait()
    for save in saves:
        save.wait()


def layer(targets, anchors, feats, halo, tiles, grads, weight):
    return pl.pallas_call(
        layer_kernel,
        out_shape=(
            jax.ShapeDtypeStruct((TGT * TILE, HID), BF16),
            jax.ShapeDtypeStruct((LOCAL, TILE, FEAT), BF16),
            jax.ShapeDtypeStruct((SRC - LOCAL, TILE, FEAT), BF16),
            jax.ShapeDtypeStruct((2 * FEAT, TILE), F32),
        ),
        in_specs=[SMEM, SMEM, ANY, ANY, ANY, ANY, VMEM],
        out_specs=(ANY, ANY, ANY, VMEM),
        scratch_shapes=[
            pltpu.VMEM((SRC, TILE, FEAT), BF16),
            pltpu.VMEM((NT, TILE, TILE), BF16),
            pltpu.VMEM((TGT * TILE, HID), BF16),
            pltpu.VMEM((TGT, TILE, FEAT), F32),
            pltpu.VMEM((TGT, FEAT, TILE), BF16),
            pltpu.VMEM((SRC, FEAT, TILE), F32),
            pltpu.VMEM((TGT * TILE, HID), BF16),
            pltpu.VMEM((SRC, TILE, FEAT), BF16),
            pltpu.VMEM((FEAT, HID), F32),
            pltpu.SemaphoreType.DMA((2,)),
            pltpu.SemaphoreType.DMA((CHUNKS,)),
            pltpu.SemaphoreType.DMA,
            pltpu.SemaphoreType.DMA((3,)),
        ],
        name="layer",
    )(targets, anchors, feats, halo, tiles, grads, weight)


def return_kernel(
    part, wpart, back, wrow,
    inbox, sums, winbox, wsums,
    own_sem, rs_send, rs_recv, send_sem, recv_sem,
):
    me_d = lax.axis_index("dom")
    me_r = lax.axis_index("rep")
    greet_all(me_d, me_r)

    def reduce_to(k):
        r = lax.rem(me_r + k, NREP)
        dev = peer_id(me_d, r)
        return (
            pltpu.make_async_remote_copy(
                src_ref=part.at[:, r], dst_ref=inbox.at[k], send_sem=rs_send.at[0, k],
                recv_sem=rs_recv.at[0, k], device_id=dev, device_id_type=MESH,
            ),
            pltpu.make_async_remote_copy(
                src_ref=wpart.at[r], dst_ref=winbox.at[k], send_sem=rs_send.at[1, k],
                recv_sem=rs_recv.at[1, k], device_id=dev, device_id_type=MESH,
            ),
        )

    for k in range(1, NREP):
        for copy in reduce_to(k):
            copy.start()
    own_halo = pltpu.make_async_copy(part.at[:, me_r], inbox.at[0], own_sem.at[0])
    own_halo.start()
    own_w = pltpu.make_async_copy(wpart.at[me_r], winbox.at[0], own_sem.at[1])
    own_w.start()
    own_halo.wait()
    own_w.wait()
    for k in range(1, NREP):
        for copy in reduce_to(k):
            copy.wait_recv()

    wsums[...] = (winbox[0] + winbox[1] + winbox[2] + winbox[3]).reshape(NDOM, 1, TILE)
    sums[...] = (
        inbox[0].astype(F32) + inbox[1].astype(F32) + inbox[2].astype(F32) + inbox[3].astype(F32)
    ).astype(BF16)

    def to(k):
        d = lax.rem(me_d + k, NDOM)
        dev = peer_id(d, me_r)
        return (
            pltpu.make_async_remote_copy(
                src_ref=sums.at[d], dst_ref=back.at[me_d], send_sem=send_sem.at[0, k],
                recv_sem=recv_sem.at[0, k], device_id=dev, device_id_type=MESH,
            ),
            pltpu.make_async_remote_copy(
                src_ref=wsums.at[d], dst_ref=wrow.at[me_d], send_sem=send_sem.at[1, k],
                recv_sem=recv_sem.at[1, k], device_id=dev, device_id_type=MESH,
            ),
        )

    def came(k):
        d = lax.rem(me_d + NDOM - k, NDOM)
        dev = peer_id(d, me_r)
        return (
            pltpu.make_async_remote_copy(
                src_ref=sums.at[d], dst_ref=back.at[d], send_sem=send_sem.at[0, k],
                recv_sem=recv_sem.at[0, k], device_id=dev, device_id_type=MESH,
            ),
            pltpu.make_async_remote_copy(
                src_ref=wsums.at[d], dst_ref=wrow.at[d], send_sem=send_sem.at[1, k],
                recv_sem=recv_sem.at[1, k], device_id=dev, device_id_type=MESH,
            ),
        )

    @pl.loop(1, NDOM)
    def _(k):
        for copy in to(k):
            copy.start()

    own_back = pltpu.make_async_copy(sums.at[me_d], back.at[me_d], own_sem.at[0])
    own_back.start()
    own_row = pltpu.make_async_copy(wsums.at[me_d], wrow.at[me_d], own_sem.at[1])
    own_row.start()
    own_back.wait()
    own_row.wait()

    @pl.loop(1, NDOM)
    def _(k):
        for copy in came(k):
            copy.wait_recv()
        for copy in to(k):
            copy.wait_send()

    for k in range(1, NREP):
        for copy in reduce_to(k):
            copy.wait_send()


def return_halo(part, wpart):
    return pl.pallas_call(
        return_kernel,
        out_shape=(
            jax.ShapeDtypeStruct((NDOM, Q, FEAT), BF16),
            jax.ShapeDtypeStruct((NDOM, 1, TILE), F32),
        ),
        in_specs=[VMEM, VMEM],
        out_specs=(VMEM, VMEM),
        scratch_shapes=[
            pltpu.VMEM((NREP, NDOM, Q, FEAT), BF16),
            pltpu.VMEM((NDOM, Q, FEAT), BF16),
            pltpu.VMEM((NREP, NDOM, TILE), F32),
            pltpu.VMEM((NDOM, 1, TILE), F32),
            pltpu.SemaphoreType.DMA((2,)),
            pltpu.SemaphoreType.DMA((2, NREP)),
            pltpu.SemaphoreType.DMA((2, NREP)),
            pltpu.SemaphoreType.DMA((2, NDOM)),
            pltpu.SemaphoreType.DMA((2, NDOM)),
        ],
        compiler_params=pltpu.CompilerParams(collective_id=1, has_side_effects=True),
        name="return_halo",
    )(part, wpart)


def scatter_kernel(rows, counts, local, back, wrow, out, wrow_out, wide, news):
    rep = lax.axis_index("rep")
    wide[pl.ds(0, ROWS), :] = local[...].astype(F32)
    wide[pl.ds(ROWS, Q), :] = jnp.zeros((Q, FEAT), F32)
    news[...] = back[...].reshape(NDOM * Q, FEAT).astype(F32)
    wrow_out[...] = jnp.sum(wrow[...], axis=0)

    @pl.loop(0, NDOM)
    def _(d):
        live = counts[0, d]
        places = []
        for c in range(Q):
            slot = rep * Q + c
            places.append(jnp.where(slot < live, rows[0, d, slot], ROWS + c))
        olds = [wide[pl.ds(row, 1), :] for row in places]
        for c, row in enumerate(places):
            wide[pl.ds(row, 1), :] = olds[c] + news[pl.ds(d * Q + c, 1), :]

    out[...] = wide[pl.ds(0, ROWS), :].astype(BF16)


def scatter_rows(rows, counts, local, back, wrow):
    return pl.pallas_call(
        scatter_kernel,
        out_shape=(
            jax.ShapeDtypeStruct((ROWS, FEAT), BF16),
            jax.ShapeDtypeStruct((1, TILE), F32),
        ),
        in_specs=[SMEM, SMEM, VMEM, VMEM, VMEM],
        out_specs=(VMEM, VMEM),
        scratch_shapes=[
            pltpu.VMEM((ROWS + Q, FEAT), F32),
            pltpu.VMEM((NDOM * Q, FEAT), F32),
        ],
        name="scatter_rows",
    )(rows, counts, local, back, wrow)


def final_kernel(
    part, wrow, out, wout, inbox,
    own_sem, rs_send, rs_recv, send_sem, recv_sem, ag_send, ag_recv,
):
    me_d = lax.axis_index("dom")
    me_r = lax.axis_index("rep")
    greet_all(me_d, me_r)

    def reduce_to(k):
        r = lax.rem(me_r + k, NREP)
        return pltpu.make_async_remote_copy(
            src_ref=part.at[r], dst_ref=inbox.at[k], send_sem=rs_send.at[k],
            recv_sem=rs_recv.at[k], device_id=peer_id(me_d, r), device_id_type=MESH,
        )

    def row_to(k):
        d = lax.rem(me_d + k, NDOM)
        return pltpu.make_async_remote_copy(
            src_ref=wrow, dst_ref=wout.at[me_r, me_d], send_sem=send_sem.at[k],
            recv_sem=recv_sem.at[k], device_id=peer_id(d, me_r), device_id_type=MESH,
        )

    def row_came(k):
        d = lax.rem(me_d + NDOM - k, NDOM)
        return pltpu.make_async_remote_copy(
            src_ref=wrow, dst_ref=wout.at[me_r, d], send_sem=send_sem.at[k],
            recv_sem=recv_sem.at[k], device_id=peer_id(d, me_r), device_id_type=MESH,
        )

    def spread(k, r):
        return pltpu.make_async_remote_copy(
            src_ref=wout.at[me_r], dst_ref=wout.at[r], send_sem=ag_send.at[k],
            recv_sem=ag_recv.at[k], device_id=peer_id(me_d, lax.rem(me_r + k, NREP)),
            device_id_type=MESH,
        )

    @pl.loop(1, NDOM)
    def _(k):
        row_to(k).start()

    for k in range(1, NREP):
        reduce_to(k).start()
    own = pltpu.make_async_copy(wrow, wout.at[me_r, me_d], own_sem)
    own.start()
    own.wait()

    @pl.loop(1, NDOM)
    def _(k):
        row_came(k).wait_recv()

    for k in range(1, NREP):
        spread(k, me_r).start()

    @pl.loop(1, NDOM)
    def _(k):
        row_to(k).wait_send()

    for k in range(1, NREP):
        reduce_to(k).wait_recv()
    out[...] = (
        part[me_r].astype(F32) + inbox[1].astype(F32) + inbox[2].astype(F32) + inbox[3].astype(F32)
    ).astype(BF16)
    for k in range(1, NREP):
        reduce_to(k).wait_send()
        spread(k, lax.rem(me_r + NREP - k, NREP)).wait_recv()
        spread(k, me_r).wait_send()


def final_sums(part, wrow):
    rows = ROWS // NREP
    return pl.pallas_call(
        final_kernel,
        out_shape=(
            jax.ShapeDtypeStruct((rows, FEAT), BF16),
            jax.ShapeDtypeStruct((NREP, NDOM, 1, TILE), F32),
        ),
        in_specs=[VMEM, VMEM],
        out_specs=(VMEM, VMEM),
        scratch_shapes=[
            pltpu.VMEM((NREP, rows, FEAT), BF16),
            pltpu.SemaphoreType.DMA,
            pltpu.SemaphoreType.DMA((NREP,)),
            pltpu.SemaphoreType.DMA((NREP,)),
            pltpu.SemaphoreType.DMA((NDOM,)),
            pltpu.SemaphoreType.DMA((NDOM,)),
            pltpu.SemaphoreType.DMA((NREP,)),
            pltpu.SemaphoreType.DMA((NREP,)),
        ],
        compiler_params=pltpu.CompilerParams(collective_id=2, has_side_effects=True),
        name="final_sums",
    )(part, wrow)


def shards(
    features, weight, out_grad, send_rows, send_count, tile_target, tile_source, tile_weights
):
    send = gather_rows(send_rows, send_count, features)
    halo = exchange_halo(send)
    activated, local, halo_grad, wpart = layer(
        tile_target,
        tile_source,
        features.reshape(LOCAL, TILE, FEAT),
        halo.reshape(SRC - LOCAL, TILE, FEAT),
        tile_weights.reshape(NT, TILE, TILE),
        out_grad,
        weight,
    )
    back, wrows = return_halo(
        halo_grad.reshape(NDOM, NREP, Q, FEAT), wpart.reshape(NREP, NDOM, TILE)
    )
    node_part, wrow = scatter_rows(
        send_rows, send_count, local.reshape(ROWS, FEAT), back, wrows
    )
    node_grad, wall = final_sums(node_part.reshape(NREP, ROWS // NREP, FEAT), wrow)
    wall = wall.reshape(2, FEAT, TILE)
    weight_grad = jnp.concatenate([wall[0], wall[1]], axis=1)
    return (activated, node_grad, weight_grad)


def solution(mesh):
    both = ("dom", "rep")
    in_specs = (
        P("dom", None),
        P(),
        P(both, None),
        P("dom", None, None),
        P("dom", None),
        P("dom", "rep", None),
        P("dom", "rep", None),
        P("dom", "rep", None, None, None),
    )
    out_specs = (P(both, None), P(both, None), P())
    return jax.shard_map(
        shards, mesh=mesh, in_specs=in_specs, out_specs=out_specs, check_vma=False
    )
```

time: 425 us -> 153 us (0.36)
  Pallas kernels: 0 us -> 149 us
  other arithmetic: 129 us -> 0.67 us
  waiting for transfers between devices: 126 us -> 0 us
  local copies, waits for them, and re-layouts: 82 us -> 2.75 us
  starting transfers between devices: 54.1 us -> 0 us
  matrix products: 30.1 us -> 0 us
    pallas_call x0 -> x6, Pallas kernels: none -> 149 us  [the longest x1 37 us: final_sums(): pl.pallas_call(final_kernel, out_shape=(jax.ShapeDtypeStruct((rows, FEAT)...]
    all_to_all x7 -> x0, waiting for transfers between devices: 126 us -> none  [the longest x2 53 us: sent_and_summed(): lax.all_to_all(pieces, axis, split_axis=0, concat_axis=0, tiled=True)]
    scatter-add x3 -> x0, other arithmetic: 109 us -> none  [the longest x1 51.8 us: shards(): jax.ops.segment_sum(backward, anchors, num_segments=src_count)]
    all_to_all x7 -> x0, starting transfers between devices: 54.1 us -> none  [the longest x2 14.6 us: from_everyone(): return lax.all_to_all(copies, axis, split_axis=0, concat_axis=0, tiled=True)]
    dot_general x2 -> x0, local copies, waits for them, and re-layouts: 34.9 us -> none  [the longest x1 17.5 us: shards(): jnp.einsum('tij,tjf->tif', values, blocks, preferred_element_type=jnp.flo...]
    gather x3 -> x0, local copies, waits for them, and re-layouts: 32.2 us -> none  [the longest x1 13 us: shards(): features[rows]]
    dot_general x5 -> x0, matrix products: 30.1 us -> none  [the longest x1 14.4 us: shards(): jnp.einsum('tij,tif->tjf', values, dblocks, preferred_element_type=jnp.fl...]
    concatenate x1, other arithmetic: 10.3 us -> 0.67 us  [shards(): weight_grad = jnp.concatenate([wall[0], wall[1]], axis=1)]
  transfers between devices with their start and end apart: 7 -> 0, of which waited for: 4 -> 0; matrix products, arithmetic and copies ran while one was open for 31% -> 0% of each run, Pallas kernels for 0% -> 0%
where the time goes in v1:
time: 153 us
  Pallas kernels  149 us (97%)
  local copies, waits for them, and re-layouts  2.75 us (2%)
    pallas_call x1, Pallas kernels, final_sums(): pl.pallas_call(final_kernel, out_shape=(jax.ShapeDtypeStruct((rows, FEAT)...  37 us
    pallas_call x1, Pallas kernels, exchange_halo(): pl.pallas_call(halo_kernel, out_shape=jax.ShapeDtypeStruct((NDOM, NREP, Q...  36.8 us
    pallas_call x1, Pallas kernels, return_halo(): pl.pallas_call(return_kernel, out_shape=(jax.ShapeDtypeStruct((NDOM, Q, F...  35.4 us
    pallas_call x1, Pallas kernels, layer(): pl.pallas_call(layer_kernel, out_shape=(jax.ShapeDtypeStruct((TGT * TILE,...  26.6 us
    pallas_call x1, Pallas kernels, scatter_rows(): pl.pallas_call(scatter_kernel, out_shape=(jax.ShapeDtypeStruct((ROWS, FEA...  7.37 us
    pallas_call x1, Pallas kernels, gather_rows(): pl.pallas_call(gather_kernel, out_shape=jax.ShapeDtypeStruct((NDOM, Q, FE...  5.64 us

profile of v1, /device:TPU:1, one launch (start us, length us, event | category | flops | bytes accessed | tf_op | source)
XLA Modules:
  0.0 153.0 jit_solution(4846727979889248483)
XLA Ops:
  0.6 5.6 %gather_rows.1.send = bf16[64,16,128]{2,1,0:T(8,128)(2,1)} custom-call(s32[1,64,64]{2,1,0:T(8,128)} %rows.3, s32[1,64]{1,0:T(1,128)} %counts.3, bf16[8192,128]{1,0:T(8,128)(2,1)} %feats.1), custom_call_target="tpu_custom_call" | custom-call | tf_op jit(solution)/shard_map/gather_rows/pallas_call | solution.py:54
  6.3 36.8 %exchange_halo.1 = bf16[64,4,16,128]{3,2,1,0:T(8,128)(2,1)} custom-call(bf16[64,16,128]{2,1,0:T(8,128)(2,1)} %gather_rows.1.send), custom_call_target="tpu_custom_call" | custom-call | tf_op jit(solution)/shard_map/exchange_halo/pallas_call | solution.py:155
  43.1 26.6 %layer.1 = (bf16[2048,256]{1,0:T(8,128)(2,1)}, bf16[64,128,128]{2,1,0:T(8,128)(2,1)}, bf16[32,128,128]{2,1,0:T(8,128)(2,1)}, f32[256,128]{1,0:T(8,128)}) custom-call(s32[1,1,256]{2,1,0:T(1,128)} %targets.1, s32[1,1,256]{2,1,0:T(1,128)} %anchors.1, bf16[64,128,128]{2,1,0:T(8,128)(2,1)} %bitcast.10, bf16[32,128,128]{2,1,0:T(8,128)(2,1)} %bitcast.11, ...), custom_call_target="tpu_custom_call" | custom-call | tf_op jit(solution)/shard_map/layer/pallas_call | solution.py:264
  69.8 35.4 %return_halo.1 = (bf16[64,16,128]{2,1,0:T(8,128)(2,1)}, f32[64,1,128]{2,1,0:T(1,128)}) custom-call(bf16[64,4,16,128]{3,2,1,0:T(8,128)(2,1)} %bitcast.14, f32[4,64,128]{2,1,0:T(8,128)} %bitcast.17), custom_call_target="tpu_custom_call" | custom-call | tf_op jit(solution)/shard_map/return_halo/pallas_call | solution.py:387
  105.2 7.4 %scatter_rows.1 = (bf16[8192,128]{1,0:T(8,128)(2,1)}, f32[1,128]{1,0:T(1,128)}) custom-call(s32[1,64,64]{2,1,0:T(8,128)} %rows.3, s32[1,64]{1,0:T(1,128)} %counts.3, bf16[8192,128]{1,0:T(8,128)(2,1)} %bitcast.13, bf16[64,16,128]{2,1,0:T(8,128)(2,1)} %get-tuple-element.17.back, f32[64,1,128]{2,1,0:T(1,128)} %get-tuple-element.18.wrow), custom_call_target="tpu_custom_call" | custom-call | tf_op jit(solution)/shard_map/scatter_rows/pallas_call | solution.py:433
  112.6 37.0 %final_sums.1 = (bf16[2048,128]{1,0:T(8,128)(2,1)}, f32[4,64,1,128]{3,2,1,0:T(1,128)}) custom-call(bf16[4,2048,128]{2,1,0:T(8,128)(2,1)} %bitcast.12, f32[1,128]{1,0:T(1,128)} %get-tuple-element.20.wrow), custom_call_target="tpu_custom_call" | custom-call | tf_op jit(solution)/shard_map/final_sums/pallas_call | solution.py:519
  149.6 0.9 fusion
  150.5 0.7 pad_maximum_fusion
  151.1 1.9 %copy.12 = bf16[2048,128]{1,0:T(8,128)(2,1)} copy(bf16[2048,128]{1,0:T(8,128)(2,1)} %get-tuple-element.29) | data formatting | bytes 1048576

commit v2 on v0

v2 whole, which is shorter than its diff:
```python
import functools

import jax
import jax.numpy as jnp
from jax import lax
from jax.experimental import pallas as pl
from jax.experimental.pallas import tpu as pltpu
from jax.sharding import PartitionSpec as P

F32 = jnp.float32
BF16 = jnp.bfloat16
TILE = 128
FEAT = 128
HID = 256
CAP = 64
NDOM = 64
NREP = 4
Q = CAP // NREP
ROWS = 8192
TGT = 16
NT = 256
SRC = 96
LOCAL = 64
CHUNKS = 16
PER = NT // CHUNKS

VMEM = pl.BlockSpec(memory_space=pltpu.VMEM)
SMEM = pl.BlockSpec(memory_space=pltpu.SMEM)
ANY = pl.BlockSpec(memory_space=pl.ANY)
MESH = pl.DeviceIdType.MESH


NZ = 8
PLANE = NDOM // NZ
HALF = PLANE // 2
PARTS = 4
DENSE = 4
SAVES = 3
LISTS = 4
PIECES = 4
WROWS = 2 * FEAT // NDOM


def place():
    me_d = lax.axis_index("dom")
    me_r = lax.axis_index("rep")
    right = lax.rem(me_r + 1, NREP)
    across = lax.rem(me_r + 2, NREP)
    left = lax.rem(me_r + 3, NREP)
    return me_d, me_r, right, across, left


def remote(src, dst, send_sem, recv_sem, dev):
    return pltpu.make_async_remote_copy(
        src_ref=src, dst_ref=dst, send_sem=send_sem, recv_sem=recv_sem,
        device_id=dev, device_id_type=MESH,
    )


def greet(devices):
    barrier = pltpu.get_barrier_semaphore()
    for dev in devices:
        pl.semaphore_signal(barrier, inc=1, device_id=dev, device_id_type=MESH)


def greet_dom(me_d, me_r):
    barrier = pltpu.get_barrier_semaphore()

    @pl.loop(1, NDOM)
    def _(k):
        pl.semaphore_signal(
            barrier, inc=1, device_id=(lax.rem(me_d + k, NDOM), me_r), device_id_type=MESH
        )


def greeted(count):
    pl.semaphore_wait(pltpu.get_barrier_semaphore(), count)


def plane_step(i):
    odd = lax.rem(i, 2)
    return lax.rem(4 + odd * ((i + 1) // 2) - (1 - odd) * (i // 2), NZ)


def near_step(i):
    return plane_step(NZ - 1 - i)


def ahead(me_d, step, place):
    z = lax.rem(me_d // PLANE + step, NZ)
    return z * PLANE + lax.rem(lax.rem(me_d, PLANE) + place, PLANE)


def behind(me_d, step, place):
    z = lax.rem(me_d // PLANE + NZ - step, NZ)
    return z * PLANE + lax.rem(lax.rem(me_d, PLANE) + PLANE - place, PLANE)


def plane_rows(me_d, step):
    return pl.ds(lax.rem(me_d // PLANE + step, NZ) * PLANE, PLANE)


OWN = NDOM - PLANE


def others(body):
    @pl.loop(0, OWN)
    def _(n):
        body(n)

    @pl.loop(OWN + 1, NDOM)
    def _(n):
        body(n)


def halo_kernel(
    rows, counts, feats, halo,
    raw, wide, picked, send,
    load_sem, own_sem, send_sem, recv_sem, ring_send, ring_recv,
):
    me_d, me_r, right, across, left = place()
    greet_dom(me_d, me_r)
    greet([(me_d, right), (me_d, left), (me_d, across)])

    load = pltpu.make_async_copy(feats, raw, load_sem)
    load.start()
    load.wait()
    wide[pl.ds(0, ROWS), :] = raw[...].astype(F32)
    wide[pl.ds(ROWS, 8), :] = jnp.zeros((8, FEAT), F32)

    @pl.loop(0, NDOM // LISTS)
    def _(g):
        for u in range(LISTS):
            d = g * LISTS + u
            live = counts[0, d]
            for c in range(Q):
                slot = me_r * Q + c
                row = jnp.where(slot < live, rows[0, d, slot], ROWS)
                picked[pl.ds(d * Q + c, 1), :] = wide[pl.ds(row, 1), :]

    send[...] = picked[...].reshape(NDOM, Q, FEAT).astype(BF16)
    greeted(NDOM - 1 + 3)

    def to(n):
        d = behind(me_d, near_step(n // PLANE), lax.rem(n, PLANE))
        return remote(
            send.at[d], halo.at[me_r, me_d], send_sem.at[n], recv_sem.at[n], (d, me_r)
        )

    def came(n):
        d = ahead(me_d, near_step(n // PLANE), lax.rem(n, PLANE))
        return remote(send.at[d], halo.at[me_r, d], send_sem.at[n], recv_sem.at[n], (d, me_r))

    own = pltpu.make_async_copy(send.at[me_d], halo.at[me_r, me_d], own_sem)
    own.start()

    @pl.loop(1, NDOM)
    def _(n):
        to(n).start()

    def share(i, k, owner):
        block = halo.at[owner, plane_rows(me_d, near_step(i))]
        dev = (me_d, lax.rem(me_r + k, NREP))
        return remote(block, block, ring_send.at[i, k], ring_recv.at[i, k], dev)

    own.wait()

    @pl.loop(0, NZ)
    def _(i):
        @pl.loop(jnp.maximum(i * PLANE, 1), (i + 1) * PLANE)
        def _(n):
            came(n).wait_recv()

        for k in (2, 1, 3):
            share(i, k, me_r).start()

    @pl.loop(1, NDOM)
    def _(n):
        to(n).wait_send()

    @pl.loop(0, NZ)
    def _(i):
        for k in range(1, NREP):
            share(i, k, lax.rem(me_r + NREP - k, NREP)).wait_recv()
            share(i, k, me_r).wait_send()


def exchange_halo(rows, counts, feats):
    return pl.pallas_call(
        halo_kernel,
        out_shape=jax.ShapeDtypeStruct((NREP, NDOM, Q, FEAT), BF16),
        in_specs=[SMEM, SMEM, ANY],
        out_specs=VMEM,
        scratch_shapes=[
            pltpu.VMEM((ROWS, FEAT), BF16),
            pltpu.VMEM((ROWS + 8, FEAT), F32),
            pltpu.VMEM((NDOM * Q, FEAT), F32),
            pltpu.VMEM((NDOM, Q, FEAT), BF16),
            pltpu.SemaphoreType.DMA,
            pltpu.SemaphoreType.DMA,
            pltpu.SemaphoreType.DMA((NDOM,)),
            pltpu.SemaphoreType.DMA((NDOM,)),
            pltpu.SemaphoreType.DMA((NZ, NREP)),
            pltpu.SemaphoreType.DMA((NZ, NREP)),
        ],
        compiler_params=pltpu.CompilerParams(collective_id=0, has_side_effects=True),
        name="exchange_halo",
    )(rows, counts, feats)


def layer_kernel(
    targets, anchors, feats, halo, tiles, grads, weight,
    act_out, sgt_out, wgrad_out,
    src, wt, og, agg, gt, sg, act, sgb, wg,
    src_sem, wt_sem, og_sem, out_sem,
):
    loads = [
        pltpu.make_async_copy(feats, src.at[pl.ds(0, 2 * LOCAL)], src_sem.at[NREP])
    ] + [
        pltpu.make_async_copy(halo.at[r], src.at[pl.ds(2 * LOCAL, NDOM), r], src_sem.at[r])
        for r in range(NREP)
    ]
    for load in loads:
        load.start()

    def tile_load(c):
        part = pl.ds(c * PER, PER)
        return pltpu.make_async_copy(tiles.at[part], wt.at[part], wt_sem.at[c])

    for c in range(CHUNKS):
        tile_load(c).start()
    grad_load = pltpu.make_async_copy(grads, og, og_sem)
    grad_load.start()

    agg[...] = jnp.zeros_like(agg)
    sg[...] = jnp.zeros_like(sg)
    wg[...] = jnp.zeros_like(wg)
    for load in loads:
        load.wait()

    @pl.loop(0, CHUNKS)
    def _(c):
        tile_load(c).wait()
        for u in range(PER):
            t = c * PER + u
            block = src[pl.ds(anchors[0, 0, t] * 2, 2)].reshape(TILE, FEAT)
            prod = jnp.dot(wt[t], block, preferred_element_type=F32)
            k = targets[0, 0, t]
            agg[k] = agg[k] + prod

    grad_load.wait()

    @pl.loop(0, TGT // DENSE)
    def _(c):
        total = wg[...]
        for u in range(DENSE):
            k = c * DENSE + u
            gathered = agg[k].astype(BF16)
            pre = jnp.dot(gathered, weight[...], preferred_element_type=F32)
            sigma = jax.nn.sigmoid(pre)
            part = pl.ds(pl.multiple_of(k * TILE, TILE), TILE)
            act[part, :] = (pre * sigma).astype(BF16)
            slope = sigma * (1.0 + pre * (1.0 - sigma))
            pre_grad = (og[part, :].astype(F32) * slope).astype(BF16)
            total += lax.dot_general(
                gathered, pre_grad, (((0,), (0,)), ((), ())), preferred_element_type=F32
            )
            gt[k] = lax.dot_general(
                weight[...], pre_grad, (((1,), (1,)), ((), ())), preferred_element_type=F32
            ).astype(BF16)
        wg[...] = total

    act_save = pltpu.make_async_copy(act, act_out, out_sem.at[0])
    act_save.start()
    wgrad_out[...] = jnp.concatenate([wg[:, :TILE], wg[:, TILE:]], axis=0)

    @pl.loop(0, CHUNKS)
    def _(c):
        for u in range(PER):
            t = c * PER + u
            prod = jnp.dot(gt[targets[0, 0, t]], wt[t], preferred_element_type=F32)
            s = anchors[0, 0, t]
            sg[s] = sg[s] + prod

    saves = []
    for i in range(SAVES):
        start = (LOCAL + i * (SRC // SAVES)) % SRC

        @pl.loop(0, SRC // SAVES // 8)
        def _(c):
            for u in range(8):
                t = start + c * 8 + u
                sgb[t] = sg[t].astype(BF16)

        part = pl.ds(start, SRC // SAVES)
        saves.append(pltpu.make_async_copy(sgb.at[part], sgt_out.at[part], out_sem.at[1 + i]))
        saves[-1].start()
    act_save.wait()
    for save in saves:
        save.wait()


def layer(targets, anchors, feats, halo, tiles, grads, weight):
    return pl.pallas_call(
        layer_kernel,
        out_shape=(
            jax.ShapeDtypeStruct((TGT * TILE, HID), BF16),
            jax.ShapeDtypeStruct((SRC, FEAT, TILE), BF16),
            jax.ShapeDtypeStruct((2 * FEAT, TILE), F32),
        ),
        in_specs=[SMEM, SMEM, ANY, ANY, ANY, ANY, VMEM],
        out_specs=(ANY, ANY, VMEM),
        scratch_shapes=[
            pltpu.VMEM((2 * SRC, NREP, Q, FEAT), BF16),
            pltpu.VMEM((NT, TILE, TILE), BF16),
            pltpu.VMEM((TGT * TILE, HID), BF16),
            pltpu.VMEM((TGT, TILE, FEAT), F32),
            pltpu.VMEM((TGT, FEAT, TILE), BF16),
            pltpu.VMEM((SRC, FEAT, TILE), F32),
            pltpu.VMEM((TGT * TILE, HID), BF16),
            pltpu.VMEM((SRC, FEAT, TILE), BF16),
            pltpu.VMEM((FEAT, HID), F32),
            pltpu.SemaphoreType.DMA((NREP + 1,)),
            pltpu.SemaphoreType.DMA((CHUNKS,)),
            pltpu.SemaphoreType.DMA,
            pltpu.SemaphoreType.DMA((1 + SAVES,)),
        ],
        name="layer",
    )(targets, anchors, feats, halo, tiles, grads, weight)


def return_kernel(
    sgt, wpart, back, local, wrows,
    turned, part, inbox, sums, wbox, wplane, wline, wsum, wsums, wtotal,
    load_sem, own_sem, ring_send, ring_recv, send_sem, recv_sem, w_send, w_recv,
):
    me_d, me_r, right, across, left = place()
    greet_dom(me_d, me_r)
    greet([(me_d, right), (me_d, left), (me_d, across)])

    halo_load = pltpu.make_async_copy(
        sgt.at[pl.ds(LOCAL, SRC - LOCAL)], turned.at[pl.ds(LOCAL, SRC - LOCAL)], load_sem.at[0]
    )
    local_load = pltpu.make_async_copy(
        sgt.at[pl.ds(0, LOCAL)], turned.at[pl.ds(0, LOCAL)], load_sem.at[1]
    )
    halo_load.start()
    local_load.start()
    one = (
        lax.broadcasted_iota(jnp.int32, (TILE, TILE), 0)
        == lax.broadcasted_iota(jnp.int32, (TILE, TILE), 1)
    ).astype(F32).astype(BF16)

    def upright(block):
        return lax.dot_general(
            one, block, (((1,), (1,)), ((), ())), preferred_element_type=F32
        ).astype(BF16)

    halo_load.wait()

    @pl.loop(0, (SRC - LOCAL) // 8)
    def _(c):
        for u in range(8):
            s = c * 8 + u
            block = upright(turned[LOCAL + s]).reshape(2, NREP, Q, FEAT)
            for r in range(NREP):
                part[r, pl.ds(s * 2, 2)] = block[:, r]

    greeted(NDOM - 1 + 3)

    def ring(i, k):
        r = lax.rem(me_r + k, NREP)
        z = plane_rows(me_d, plane_step(i))
        return remote(
            part.at[r, z], inbox.at[k, z], ring_send.at[i, k], ring_recv.at[i, k], (me_d, r)
        )

    me_z, me_p = me_d // PLANE, lax.rem(me_d, PLANE)

    def in_plane(src, dst, k, stage, back_from):
        p = lax.rem(me_p + k, PLANE)
        q = lax.rem(me_p + PLANE - k, PLANE) if back_from else me_p
        return remote(
            src(p), dst(q, k), w_send.at[stage, k], w_recv.at[stage, k], (me_z * PLANE + p, me_r)
        )

    def along_z(src, dst, k, stage, back_from):
        z = lax.rem(me_z + k, NZ)
        y = lax.rem(me_z + NZ - k, NZ) if back_from else me_z
        return remote(
            src(z), dst(y, k), w_send.at[stage, k], w_recv.at[stage, k], (z * PLANE + me_p, me_r)
        )

    def w_stage(stage, k, back_from=False):
        if stage == 0:
            return in_plane(
                lambda p: wpart.at[pl.ds(p * NZ, NZ)], lambda q, k: wbox.at[k], k, 0, back_from
            )
        if stage == 1:
            return along_z(lambda z: wplane.at[z], lambda y, k: wline.at[k], k, 1, back_from)
        if stage == 2:
            r = lax.rem(me_r + k, NREP)
            return remote(wsum, wsums.at[k], w_send.at[2, k], w_recv.at[2, k], (me_d, r))
        if stage == 3:
            return along_z(
                lambda z: wtotal, lambda y, k: wrows.at[me_p * NZ + y], k, 3, back_from
            )
        mine = wrows.at[pl.ds(me_p * NZ, NZ)]
        return in_plane(
            lambda p: mine, lambda q, k: wrows.at[pl.ds(q * NZ, NZ)], k, 4, back_from
        )

    peers = (PLANE, NZ, NREP, NZ, PLANE)

    def w_start(stage):
        for k in range(1, peers[stage]):
            w_stage(stage, k).start()

    def w_wait(stage):
        for k in range(1, peers[stage]):
            w_stage(stage, k, True).wait_recv()

    def to(n):
        d = ahead(me_d, plane_step(n // PLANE), lax.rem(n, PLANE))
        return remote(sums.at[d], back.at[me_d], send_sem.at[n], recv_sem.at[n], (d, me_r))

    def came(n):
        d = behind(me_d, plane_step(n // PLANE), lax.rem(n, PLANE))
        return remote(sums.at[d], back.at[d], send_sem.at[n], recv_sem.at[n], (d, me_r))

    @pl.loop(0, NZ)
    def _(i):
        for k in (2, 1, 3):
            ring(i, k).start()

    w_start(0)
    local_load.wait()

    @pl.loop(0, LOCAL // 8)
    def _(i):
        for u in range(8):
            local[i * 8 + u] = upright(turned[i * 8 + u])

    def finish(i):
        for k in range(1, NREP):
            ring(i, k).wait_recv()
        z = plane_rows(me_d, plane_step(i))
        sums[z] = (
            (part[me_r, z].astype(F32) + inbox[1, z].astype(F32))
            + (inbox[2, z].astype(F32) + inbox[3, z].astype(F32))
        ).astype(BF16)

        @pl.loop(i * PLANE, jnp.minimum((i + 1) * PLANE, NDOM))
        def _(n):
            @pl.when(n != OWN)
            def _():
                to(n).start()

    w_wait(0)
    wbox[0] = wpart[pl.ds(me_p * NZ, NZ)]
    wplane[...] = jnp.sum(wbox[...], axis=0)
    w_start(1)

    @pl.loop(0, 3)
    def _(i):
        finish(i)

    w_wait(1)
    wline[0] = wplane[me_z]
    wsum[...] = jnp.sum(wline[...], axis=0)
    w_start(2)
    finish(3)
    finish(4)
    w_wait(2)
    wsums[0] = wsum[...]
    terms = [wsums[lax.rem(NREP + me_r - r, NREP)] for r in range(NREP)]
    wtotal[...] = (terms[0] + terms[1]) + (terms[2] + terms[3])
    wrows[me_p * NZ + me_z] = wtotal[...]
    w_start(3)
    finish(5)
    finish(6)
    finish(7)
    own = pltpu.make_async_copy(sums.at[me_d], back.at[me_d], own_sem.at[0])
    own.start()
    w_wait(3)
    w_start(4)
    own.wait()
    others(lambda n: came(n).wait_recv())
    w_wait(4)
    others(lambda n: to(n).wait_send())
    for stage in range(5):
        for k in range(1, peers[stage]):
            w_stage(stage, k).wait_send()

    @pl.loop(0, NZ)
    def _(i):
        for k in range(1, NREP):
            ring(i, k).wait_send()


def return_halo(sgt, wpart):
    dma = pltpu.SemaphoreType.DMA
    return pl.pallas_call(
        return_kernel,
        out_shape=(
            jax.ShapeDtypeStruct((NDOM, Q, FEAT), BF16),
            jax.ShapeDtypeStruct((LOCAL, TILE, FEAT), BF16),
            jax.ShapeDtypeStruct((NDOM, WROWS, TILE), F32),
        ),
        in_specs=[ANY, VMEM],
        out_specs=(VMEM, VMEM, VMEM),
        scratch_shapes=[
            pltpu.VMEM((SRC, FEAT, TILE), BF16),
            pltpu.VMEM((NREP, NDOM, Q, FEAT), BF16),
            pltpu.VMEM((NREP, NDOM, Q, FEAT), BF16),
            pltpu.VMEM((NDOM, Q, FEAT), BF16),
            pltpu.VMEM((PLANE, NZ, WROWS, TILE), F32),
            pltpu.VMEM((NZ, WROWS, TILE), F32),
            pltpu.VMEM((NZ, WROWS, TILE), F32),
            pltpu.VMEM((WROWS, TILE), F32),
            pltpu.VMEM((NREP, WROWS, TILE), F32),
            pltpu.VMEM((WROWS, TILE), F32),
            dma((2,)),
            dma((1,)),
            dma((NZ, NREP)),
            dma((NZ, NREP)),
            dma((NDOM,)),
            dma((NDOM,)),
            dma((5, PLANE)),
            dma((5, PLANE)),
        ],
        compiler_params=pltpu.CompilerParams(collective_id=1, has_side_effects=True),
        name="return_halo",
    )(sgt, wpart)


def scatter_kernel(rows, counts, local, back, out, raw, wide, news, done, in_sem, out_sem):
    rep = lax.axis_index("rep")
    size = ROWS // PIECES
    loads = [
        pltpu.make_async_copy(
            local.at[pl.ds(i * size, size)], raw.at[pl.ds(i * size, size)], in_sem.at[i]
        )
        for i in range(PIECES)
    ]
    for load in loads:
        load.start()
    wide[pl.ds(ROWS, Q), :] = jnp.zeros((Q, FEAT), F32)
    news[...] = back[...].reshape(NDOM * Q, FEAT).astype(F32)
    for i in range(PIECES):
        loads[i].wait()
        wide[pl.ds(i * size, size), :] = raw[pl.ds(i * size, size), :].astype(F32)

    @pl.loop(0, NDOM // LISTS)
    def _(g):
        for u in range(LISTS):
            d = g * LISTS + u
            live = counts[0, d]
            places = []
            for c in range(Q):
                slot = rep * Q + c
                places.append(jnp.where(slot < live, rows[0, d, slot], ROWS + c))
            olds = [wide[pl.ds(row, 1), :] for row in places]
            for c, row in enumerate(places):
                wide[pl.ds(row, 1), :] = olds[c] + news[pl.ds(d * Q + c, 1), :]

    saves = []
    for i in range(PIECES):
        part = pl.ds(i * size, size)
        done[part, :] = wide[part, :].astype(BF16)
        saves.append(pltpu.make_async_copy(done.at[part], out.at[part], out_sem.at[i]))
        saves[-1].start()
    for save in saves:
        save.wait()


def scatter_rows(rows, counts, local, back):
    return pl.pallas_call(
        scatter_kernel,
        out_shape=jax.ShapeDtypeStruct((ROWS, FEAT), BF16),
        in_specs=[SMEM, SMEM, ANY, VMEM],
        out_specs=ANY,
        scratch_shapes=[
            pltpu.VMEM((ROWS, FEAT), BF16),
            pltpu.VMEM((ROWS + Q, FEAT), F32),
            pltpu.VMEM((NDOM * Q, FEAT), F32),
            pltpu.VMEM((ROWS, FEAT), BF16),
            pltpu.SemaphoreType.DMA((PIECES,)),
            pltpu.SemaphoreType.DMA((PIECES,)),
        ],
        name="scatter_rows",
    )(rows, counts, local, back)


def final_kernel(
    part, inbox, held, mid, relayed, load_sem, ring_send, ring_recv,
):
    me_d, me_r, right, across, left = place()
    greet([(me_d, right), (me_d, left)])
    loads = [
        pltpu.make_async_copy(part.at[r], held.at[r], load_sem.at[i])
        for i, r in enumerate((across, right, left))
    ]
    for load in loads:
        load.start()
    size = ROWS // NREP // PARTS // 2

    def ring(i, j):
        a = pl.ds(i * 2 * size, size)
        b = pl.ds(i * 2 * size + size, size)
        src, dst, dev = (
            (held.at[across, a], mid.at[0, i], right),
            (held.at[across, b], mid.at[1, i], left),
            (held.at[right, b], inbox.at[0, b], right),
            (held.at[left, a], inbox.at[1, a], left),
            (relayed.at[0, i], inbox.at[0, a], right),
            (relayed.at[1, i], inbox.at[1, b], left),
        )[j]
        return remote(src, dst, ring_send.at[i, j], ring_recv.at[i, j], (me_d, dev))

    def relay(i):
        a = pl.ds(i * 2 * size, size)
        b = pl.ds(i * 2 * size + size, size)
        ring(i, 0).wait_recv()
        relayed[0, i] = (mid[0, i].astype(F32) + held[right, a].astype(F32)).astype(BF16)
        ring(i, 1).wait_recv()
        relayed[1, i] = (mid[1, i].astype(F32) + held[left, b].astype(F32)).astype(BF16)
        ring(i, 4).start()
        ring(i, 5).start()

    for load in loads:
        load.wait()
    greeted(2)
    for j in range(4):
        ring(0, j).start()
    for i in range(PARTS):
        if i + 1 < PARTS:
            for j in range(4):
                ring(i + 1, j).start()
        relay(i)
    for i in range(PARTS):
        for j in range(2, 6):
            ring(i, j).wait_recv()
    for i in range(PARTS):
        for j in range(6):
            ring(i, j).wait_send()


def final_sums(part):
    rows = ROWS // NREP
    dma = pltpu.SemaphoreType.DMA
    return pl.pallas_call(
        final_kernel,
        out_shape=jax.ShapeDtypeStruct((2, rows, FEAT), BF16),
        in_specs=[ANY],
        out_specs=VMEM,
        scratch_shapes=[
            pltpu.VMEM((NREP, rows, FEAT), BF16),
            pltpu.VMEM((2, PARTS, rows // PARTS // 2, FEAT), BF16),
            pltpu.VMEM((2, PARTS, rows // PARTS // 2, FEAT), BF16),
            dma((3,)),
            dma((PARTS, 6)),
            dma((PARTS, 6)),
        ],
        compiler_params=pltpu.CompilerParams(collective_id=2, has_side_effects=True),
        name="final_sums",
    )(part)


def shards(
    features, weight, out_grad, send_rows, send_count, tile_target, tile_source, tile_weights
):
    halo = exchange_halo(send_rows, send_count, features)
    activated, sgt, wpart = layer(
        tile_target,
        tile_source,
        features.reshape(2 * LOCAL, NREP, Q, FEAT),
        halo,
        tile_weights.reshape(NT, TILE, TILE),
        out_grad,
        weight,
    )
    back, local, wrows = return_halo(sgt, wpart.reshape(NDOM, WROWS, TILE))
    node_part = scatter_rows(send_rows, send_count, local.reshape(ROWS, FEAT), back)
    node_part = node_part.reshape(NREP, ROWS // NREP, FEAT)
    sums = final_sums(node_part)
    own = lax.dynamic_index_in_dim(node_part, lax.axis_index("rep"), 0, keepdims=False)
    node_grad = (own.astype(F32) + sums[0].astype(F32) + sums[1].astype(F32)).astype(BF16)
    weight_grad = wrows.reshape(2, FEAT, TILE).transpose(1, 0, 2).reshape(FEAT, 2 * TILE)
    return (activated, node_grad, weight_grad)


def solution(mesh):
    both = ("dom", "rep")
    in_specs = (
        P("dom", None),
        P(),
        P(both, None),
        P("dom", None, None),
        P("dom", None),
        P("dom", "rep", None),
        P("dom", "rep", None),
        P("dom", "rep", None, None, None),
    )
    out_specs = (P(both, None), P(both, None), P())
    return jax.shard_map(
        shards, mesh=mesh, in_specs=in_specs, out_specs=out_specs, check_vma=False
    )
```

time: 425 us -> 122 us (0.29)
  other arithmetic: 129 us -> 2.36 us
  waiting for transfers between devices: 126 us -> 0 us
  Pallas kernels: 0 us -> 118 us
  local copies, waits for them, and re-layouts: 82 us -> 0.67 us
  starting transfers between devices: 54.1 us -> 0 us
  matrix products: 30.1 us -> 0 us
    all_to_all x7 -> x0, waiting for transfers between devices: 126 us -> none  [the longest x2 53 us: sent_and_summed(): lax.all_to_all(pieces, axis, split_axis=0, concat_axis=0, tiled=True)]
    pallas_call x0 -> x5, Pallas kernels: none -> 118 us  [the longest x1 33.7 us: exchange_halo(): pl.pallas_call(halo_kernel, out_shape=jax.ShapeDtypeStruct((NREP, NDOM, Q...]
    scatter-add x3 -> x0, other arithmetic: 109 us -> none  [the longest x1 51.8 us: shards(): jax.ops.segment_sum(backward, anchors, num_segments=src_count)]
    all_to_all x7 -> x0, starting transfers between devices: 54.1 us -> none  [the longest x2 14.6 us: from_everyone(): return lax.all_to_all(copies, axis, split_axis=0, concat_axis=0, tiled=True)]
    dot_general x2 -> x0, local copies, waits for them, and re-layouts: 34.9 us -> none  [the longest x1 17.5 us: shards(): jnp.einsum('tij,tjf->tif', values, blocks, preferred_element_type=jnp.flo...]
    gather x3 -> x0, local copies, waits for them, and re-layouts: 32.2 us -> none  [the longest x1 13 us: shards(): features[rows]]
    dot_general x5 -> x0, matrix products: 30.1 us -> none  [the longest x1 14.4 us: shards(): jnp.einsum('tij,tif->tjf', values, dblocks, preferred_element_type=jnp.fl...]
    concatenate x1 -> x0, other arithmetic: 10.3 us -> none  [shards(): sources = jnp.concatenate([features, halo.reshape(-1, feat)], axis=0)]
  transfers between devices with their start and end apart: 7 -> 0, of which waited for: 4 -> 0; matrix products, arithmetic and copies ran while one was open for 31% -> 0% of each run, Pallas kernels for 0% -> 0%
where the time goes in v2:
time: 122 us; the launch traced here: 121 us
  Pallas kernels  118 us (97%)
  other arithmetic  2.36 us (2%)
    pallas_call x1, Pallas kernels, exchange_halo(): pl.pallas_call(halo_kernel, out_shape=jax.ShapeDtypeStruct((NREP, NDOM, Q...  33.7 us
    pallas_call x1, Pallas kernels, return_halo(): pl.pallas_call(return_kernel, out_shape=(jax.ShapeDtypeStruct((NDOM, Q, F...  33.2 us
    pallas_call x1, Pallas kernels, final_sums(): pl.pallas_call(final_kernel, out_shape=jax.ShapeDtypeStruct((2, rows, FEA...  21.8 us
    pallas_call x1, Pallas kernels, layer(): pl.pallas_call(layer_kernel, out_shape=(jax.ShapeDtypeStruct((TGT * TILE,...  21.3 us
    pallas_call x1, Pallas kernels, scatter_rows(): pl.pallas_call(scatter_kernel, out_shape=jax.ShapeDtypeStruct((ROWS, FEAT...  7.83 us

profile of v2, /device:TPU:1, one launch (start us, length us, event | category | flops | bytes accessed | tf_op | source)
XLA Modules:
  0.0 121.5 jit_solution(18111125925790802177)
XLA Ops:
  0.6 33.7 %exchange_halo.1.halo = bf16[4,64,16,128]{3,2,1,0:T(8,128)(2,1)} custom-call(s32[1,64,64]{2,1,0:T(8,128)} %rows.3, s32[1,64]{1,0:T(1,128)} %counts.3, bf16[8192,128]{1,0:T(8,128)(2,1)} %feats.1), custom_call_target="tpu_custom_call" | custom-call | tf_op jit(solution)/shard_map/exchange_halo/pallas_call | solution.py:189
  34.3 21.3 %layer.1 = (bf16[2048,256]{1,0:T(8,128)(2,1)}, bf16[96,128,128]{2,1,0:T(8,128)(2,1)}, f32[256,128]{1,0:T(8,128)}) custom-call(s32[1,1,256]{2,1,0:T(1,128)} %targets.1, s32[1,1,256]{2,1,0:T(1,128)} %anchors.1, bf16[128,4,16,128]{3,2,1,0:T(8,128)(2,1)} %bitcast.17, bf16[4,64,16,128]{3,2,1,0:T(8,128)(2,1)} %exchange_halo.1.halo, ...), custom_call_target="tpu_custom_call" | custom-call | tf_op jit(solution)/shard_map/layer/pallas_call | solution.py:304
  55.6 33.2 %return_halo.1 = (bf16[64,16,128]{2,1,0:T(8,128)(2,1)}, bf16[64,128,128]{2,1,0:T(8,128)(2,1)}, f32[64,4,128]{2,1,0:T(4,128)}) custom-call(bf16[96,128,128]{2,1,0:T(8,128)(2,1)} %get-tuple-element.10.sgt, f32[64,4,128]{2,1,0:T(4,128)} %bitcast.19), custom_call_target="tpu_custom_call" | custom-call | tf_op jit(solution)/shard_map/return_halo/pallas_call | solution.py:503
  88.8 7.8 %scatter_rows.1 = bf16[8192,128]{1,0:T(8,128)(2,1)} custom-call(s32[1,64,64]{2,1,0:T(8,128)} %rows.3, s32[1,64]{1,0:T(1,128)} %counts.3, bf16[8192,128]{1,0:T(8,128)(2,1)} %bitcast.18, bf16[64,16,128]{2,1,0:T(8,128)(2,1)} %get-tuple-element.13.back), custom_call_target="tpu_custom_call" | custom-call | tf_op jit(solution)/shard_map/scatter_rows/pallas_call | solution.py:578
  96.6 0.0 copy-start
  96.6 21.8 %final_sums.1 = bf16[2,2048,128]{2,1,0:T(8,128)(2,1)} custom-call(bf16[4,2048,128]{2,1,0:T(8,128)(2,1)} %bitcast.14), custom_call_target="tpu_custom_call" | custom-call | tf_op jit(solution)/shard_map/final_sums/pallas_call | solution.py:652
  118.4 2.4 %fusion = bf16[2048,128]{1,0:T(8,128)(2,1)} fusion(bf16[2,2048,128]{2,1,0:T(8,128)(2,1)} %final_sums.1, bf16[4,2048,128]{2,1,0:T(8,128)(2,1)} %bitcast.15, s32[]{:T(128)S(6)} %select_n.4), kind=kLoop, calls=%fused_computation.1 | loop fusion | flops 1572864 | bytes 2097156 | tf_op jit(solution)/shard_map/convert_element_type | solution.py:688
  120.8 0.0 copy-done
  120.8 0.7 copy.14
Async XLA Ops:
  96.6 24.2 %copy-start = (f32[64,4,128]{2,1,0:T(4,128)S(1)}, f32[64,4,128]{2,1,0:T(4,128)}, u32[]{:S(2)}) copy-start(f32[64,4,128]{2,1,0:T(4,128)} %get-tuple-element.14) | copy-start | bytes 393220

commit v3 on v2

--- a/solution.py
+++ b/solution.py
@@ -27,6 +27,14 @@
 VMEM = pl.BlockSpec(memory_space=pltpu.VMEM)
 SMEM = pl.BlockSpec(memory_space=pltpu.SMEM)
 ANY = pl.BlockSpec(memory_space=pl.ANY)
+HBM = pl.BlockSpec(memory_space=pltpu.HBM)
+
+
+def busy(micros):
+    return pl.CostEstimate(
+        flops=micros * 400_000_000, bytes_accessed=micros * 3_000_000, transcendentals=0
+    )
+
 MESH = pl.DeviceIdType.MESH
 
 
@@ -34,10 +42,12 @@
 PLANE = NDOM // NZ
 HALF = PLANE // 2
 PARTS = 4
-DENSE = 4
+DENSE = 8
 SAVES = 3
-LISTS = 4
+LISTS = 2
 PIECES = 4
+LAG = 3
+RELAYED = 6
 WROWS = 2 * FEAT // NDOM
 
 
@@ -66,11 +76,19 @@
 def greet_dom(me_d, me_r):
     barrier = pltpu.get_barrier_semaphore()
 
-    @pl.loop(1, NDOM)
-    def _(k):
-        pl.semaphore_signal(
-            barrier, inc=1, device_id=(lax.rem(me_d + k, NDOM), me_r), device_id_type=MESH
-        )
+    after, _ = places_around(me_d)
+
+    def hail(z, p):
+        pl.semaphore_signal(barrier, inc=1, device_id=(z + p, me_r), device_id_type=MESH)
+
+    for p in after[1:]:
+        hail(plane_at(me_d, 0), p)
+
+    @pl.loop(1, NZ)
+    def _(i):
+        z = plane_at(me_d, i)
+        for p in after:
+            hail(z, p)
 
 
 def greeted(count):
@@ -86,36 +104,24 @@
     return plane_step(NZ - 1 - i)
 
 
-def ahead(me_d, step, place):
-    z = lax.rem(me_d // PLANE + step, NZ)
-    return z * PLANE + lax.rem(lax.rem(me_d, PLANE) + place, PLANE)
-
-
-def behind(me_d, step, place):
-    z = lax.rem(me_d // PLANE + NZ - step, NZ)
-    return z * PLANE + lax.rem(lax.rem(me_d, PLANE) + PLANE - place, PLANE)
+def plane_at(me_d, step):
+    return lax.rem(me_d // PLANE + step, NZ) * PLANE
 
 
 def plane_rows(me_d, step):
-    return pl.ds(lax.rem(me_d // PLANE + step, NZ) * PLANE, PLANE)
-
-
-OWN = NDOM - PLANE
-
-
-def others(body):
-    @pl.loop(0, OWN)
-    def _(n):
-        body(n)
-
-    @pl.loop(OWN + 1, NDOM)
-    def _(n):
-        body(n)
+    return pl.ds(plane_at(me_d, step), PLANE)
+
+
+def places_around(me_d):
+    me_p = lax.rem(me_d, PLANE)
+    after = [lax.rem(me_p + k, PLANE) for k in range(PLANE)]
+    before = [lax.rem(me_p + PLANE - k, PLANE) for k in range(PLANE)]
+    return after, before
 
 
 def halo_kernel(
-    rows, counts, feats, halo,
-    raw, wide, picked, send,
+    rows_in, counts_in, feats, halo,
+    rows, counts, raw, wide, picked, send, list_sem,
     load_sem, own_sem, send_sem, recv_sem, ring_send, ring_recv,
 ):
     me_d, me_r, right, across, left = place()
@@ -124,86 +130,151 @@
 
     load = pltpu.make_async_copy(feats, raw, load_sem)
     load.start()
+    lists = [
+        pltpu.make_async_copy(rows_in, rows, list_sem.at[0]),
+        pltpu.make_async_copy(counts_in, counts, list_sem.at[1]),
+    ]
+    for part in lists:
+        part.start()
     load.wait()
     wide[pl.ds(0, ROWS), :] = raw[...].astype(F32)
     wide[pl.ds(ROWS, 8), :] = jnp.zeros((8, FEAT), F32)
-
-    @pl.loop(0, NDOM // LISTS)
-    def _(g):
-        for u in range(LISTS):
-            d = g * LISTS + u
-            live = counts[0, d]
-            for c in range(Q):
-                slot = me_r * Q + c
-                row = jnp.where(slot < live, rows[0, d, slot], ROWS)
-                picked[pl.ds(d * Q + c, 1), :] = wide[pl.ds(row, 1), :]
+    for part in lists:
+        part.wait()
+
+    for r in range(NREP):
+
+        @pl.when(me_r == r)
+        def _():
+            @pl.loop(0, NDOM // LISTS)
+            def _(g):
+                for u in range(LISTS):
+                    d = g * LISTS + u
+                    live = counts[0, d]
+                    for c in range(Q):
+                        row = jnp.where(r * Q + c < live, rows[0, d, r * Q + c], ROWS)
+                        picked[pl.ds(d * Q + c, 1), :] = wide[pl.ds(row, 1), :]
 
     send[...] = picked[...].reshape(NDOM, Q, FEAT).astype(BF16)
     greeted(NDOM - 1 + 3)
 
-    def to(n):
-        d = behind(me_d, near_step(n // PLANE), lax.rem(n, PLANE))
+    after, before = places_around(me_d)
+
+    def to(i, k):
+        d = plane_at(me_d, NZ - near_step(i)) + before[k]
+        n = i * PLANE + k
         return remote(
             send.at[d], halo.at[me_r, me_d], send_sem.at[n], recv_sem.at[n], (d, me_r)
         )
 
-    def came(n):
-        d = ahead(me_d, near_step(n // PLANE), lax.rem(n, PLANE))
+    def came(i, k):
+        d = plane_at(me_d, near_step(i)) + after[k]
+        n = i * PLANE + k
         return remote(send.at[d], halo.at[me_r, d], send_sem.at[n], recv_sem.at[n], (d, me_r))
+
+    for k in range(1, PLANE):
+        to(0, k).start()
+
+    @pl.loop(1, NZ)
+    def _(i):
+        for k in range(PLANE):
+            to(i, k).start()
 
     own = pltpu.make_async_copy(send.at[me_d], halo.at[me_r, me_d], own_sem)
     own.start()
 
-    @pl.loop(1, NDOM)
-    def _(n):
-        to(n).start()
-
-    def share(i, k, owner):
-        block = halo.at[owner, plane_rows(me_d, near_step(i))]
-        dev = (me_d, lax.rem(me_r + k, NREP))
-        return remote(block, block, ring_send.at[i, k], ring_recv.at[i, k], dev)
+    def ring(i, j, owner):
+        z = plane_at(me_d, near_step(i))
+        skip, size = ((0, PLANE), (0, PLANE), (0, HALF), (HALF, HALF), (0, PLANE))[j]
+        block = halo.at[owner, pl.ds(z + skip, size)]
+        dev = (me_d, (right, left, right, left, across)[j])
+        return remote(block, block, ring_send.at[i, j], ring_recv.at[i, j], dev)
+
+    def first(i):
+        ring(i, 0, me_r).start()
+        ring(i, 1, me_r).start()
+
+    def relay(i):
+        ring(i, 0, left).wait_recv()
+        ring(i, 2, left).start()
+        ring(i, 1, right).wait_recv()
+        ring(i, 3, right).start()
+
+    def arrived(i):
+        for k in range(PLANE):
+            came(i, k).wait_recv()
 
     own.wait()
-
-    @pl.loop(0, NZ)
-    def _(i):
-        @pl.loop(jnp.maximum(i * PLANE, 1), (i + 1) * PLANE)
-        def _(n):
-            came(n).wait_recv()
-
-        for k in (2, 1, 3):
-            share(i, k, me_r).start()
-
-    @pl.loop(1, NDOM)
-    def _(n):
-        to(n).wait_send()
-
-    @pl.loop(0, NZ)
-    def _(i):
-        for k in range(1, NREP):
-            share(i, k, lax.rem(me_r + NREP - k, NREP)).wait_recv()
-            share(i, k, me_r).wait_send()
+    for k in range(1, PLANE):
+        came(0, k).wait_recv()
+    first(0)
+    for i in range(1, LAG):
+        arrived(i)
+        first(i)
+
+    @pl.loop(LAG, RELAYED)
+    def _(i):
+        arrived(i)
+        first(i)
+        relay(i - LAG)
+
+    @pl.loop(RELAYED, NZ)
+    def _(i):
+        arrived(i)
+        ring(i, 4, me_r).start()
+        first(i)
+
+    @pl.loop(RELAYED - LAG, RELAYED)
+    def _(i):
+        relay(i)
+
+    for k in range(1, PLANE):
+        to(0, k).wait_send()
+
+    @pl.loop(1, NZ)
+    def _(i):
+        for k in range(PLANE):
+            to(i, k).wait_send()
+
+    @pl.loop(0, RELAYED)
+    def _(i):
+        ring(i, 2, across).wait_recv()
+        ring(i, 3, across).wait_recv()
+        for j in range(4):
+            ring(i, j, me_r).wait_send()
+
+    @pl.loop(RELAYED, NZ)
+    def _(i):
+        ring(i, 0, left).wait_recv()
+        ring(i, 1, right).wait_recv()
+        ring(i, 4, across).wait_recv()
+        for j in (0, 1, 4):
+            ring(i, j, me_r).wait_send()
 
 
 def exchange_halo(rows, counts, feats):
     return pl.pallas_call(
         halo_kernel,
         out_shape=jax.ShapeDtypeStruct((NREP, NDOM, Q, FEAT), BF16),
-        in_specs=[SMEM, SMEM, ANY],
+        in_specs=[HBM, HBM, HBM],
         out_specs=VMEM,
+        cost_estimate=busy(24),
         scratch_shapes=[
+            pltpu.SMEM((1, NDOM, CAP), jnp.int32),
+            pltpu.SMEM((1, NDOM), jnp.int32),
             pltpu.VMEM((ROWS, FEAT), BF16),
             pltpu.VMEM((ROWS + 8, FEAT), F32),
             pltpu.VMEM((NDOM * Q, FEAT), F32),
             pltpu.VMEM((NDOM, Q, FEAT), BF16),
+            pltpu.SemaphoreType.DMA((2,)),
             pltpu.SemaphoreType.DMA,
             pltpu.SemaphoreType.DMA,
             pltpu.SemaphoreType.DMA((NDOM,)),
             pltpu.SemaphoreType.DMA((NDOM,)),
-            pltpu.SemaphoreType.DMA((NZ, NREP)),
-            pltpu.SemaphoreType.DMA((NZ, NREP)),
+            pltpu.SemaphoreType.DMA((NZ, 5)),
+            pltpu.SemaphoreType.DMA((NZ, 5)),
         ],
-        compiler_params=pltpu.CompilerParams(collective_id=0, has_side_effects=True),
+        compiler_params=pltpu.CompilerParams(collective_id=0, has_side_effects=True, vmem_limit_bytes=14 << 20),
         name="exchange_halo",
     )(rows, counts, feats)
 
@@ -325,13 +396,15 @@
             pltpu.SemaphoreType.DMA,
             pltpu.SemaphoreType.DMA((1 + SAVES,)),
         ],
+        compiler_params=pltpu.CompilerParams(vmem_limit_bytes=30 << 20),
+        cost_estimate=busy(16),
         name="layer",
     )(targets, anchors, feats, halo, tiles, grads, weight)
 
 
 def return_kernel(
-    sgt, wpart, back, local, wrows,
-    turned, part, inbox, sums, wbox, wplane, wline, wsum, wsums, wtotal,
+    sgt, wpart, back, local, wtotal,
+    turned, part, inbox, sums, wbox, wplane, wline, wsum, wsums, upright_local,
     load_sem, own_sem, ring_send, ring_recv, send_sem, recv_sem, w_send, w_recv,
 ):
     me_d, me_r, right, across, left = place()
@@ -398,19 +471,10 @@
             )
         if stage == 1:
             return along_z(lambda z: wplane.at[z], lambda y, k: wline.at[k], k, 1, back_from)
-        if stage == 2:
-            r = lax.rem(me_r + k, NREP)
-            return remote(wsum, wsums.at[k], w_send.at[2, k], w_recv.at[2, k], (me_d, r))
-        if stage == 3:
-            return along_z(
-                lambda z: wtotal, lambda y, k: wrows.at[me_p * NZ + y], k, 3, back_from
-            )
-        mine = wrows.at[pl.ds(me_p * NZ, NZ)]
-        return in_plane(
-            lambda p: mine, lambda q, k: wrows.at[pl.ds(q * NZ, NZ)], k, 4, back_from
-        )
-
-    peers = (PLANE, NZ, NREP, NZ, PLANE)
+        r = lax.rem(me_r + k, NREP)
+        return remote(wsum, wsums.at[k], w_send.at[2, k], w_recv.at[2, k], (me_d, r))
+
+    peers = (PLANE, NZ, NREP)
 
     def w_start(stage):
         for k in range(1, peers[stage]):
@@ -420,13 +484,26 @@
         for k in range(1, peers[stage]):
             w_stage(stage, k, True).wait_recv()
 
-    def to(n):
-        d = ahead(me_d, plane_step(n // PLANE), lax.rem(n, PLANE))
+    after, before = places_around(me_d)
+
+    def to(i, k):
+        d = plane_at(me_d, plane_step(i)) + after[k]
+        n = i * PLANE + k
         return remote(sums.at[d], back.at[me_d], send_sem.at[n], recv_sem.at[n], (d, me_r))
 
-    def came(n):
-        d = behind(me_d, plane_step(n // PLANE), lax.rem(n, PLANE))
+    def came(i, k):
+        d = plane_at(me_d, NZ - plane_step(i)) + before[k]
+        n = i * PLANE + k
         return remote(sums.at[d], back.at[d], send_sem.at[n], recv_sem.at[n], (d, me_r))
+
+    def others(body):
+        @pl.loop(0, NZ - 1)
+        def _(i):
+            for k in range(PLANE):
+                body(i, k)
+
+        for k in range(1, PLANE):
+            body(NZ - 1, k)
 
     @pl.loop(0, NZ)
     def _(i):
@@ -439,9 +516,12 @@
     @pl.loop(0, LOCAL // 8)
     def _(i):
         for u in range(8):
-            local[i * 8 + u] = upright(turned[i * 8 + u])
-
-    def finish(i):
+            upright_local[i * 8 + u] = upright(turned[i * 8 + u])
+
+    local_save = pltpu.make_async_copy(upright_local, local, own_sem.at[1])
+    local_save.start()
+
+    def finish(i, last=False):
         for k in range(1, NREP):
             ring(i, k).wait_recv()
         z = plane_rows(me_d, plane_step(i))
@@ -449,12 +529,8 @@
             (part[me_r, z].astype(F32) + inbox[1, z].astype(F32))
             + (inbox[2, z].astype(F32) + inbox[3, z].astype(F32))
         ).astype(BF16)
-
-        @pl.loop(i * PLANE, jnp.minimum((i + 1) * PLANE, NDOM))
-        def _(n):
-            @pl.when(n != OWN)
-            def _():
-                to(n).start()
+        for k in range(1 if last else 0, PLANE):
+            to(i, k).start()
 
     w_wait(0)
     wbox[0] = wpart[pl.ds(me_p * NZ, NZ)]
@@ -471,24 +547,20 @@
     w_start(2)
     finish(3)
     finish(4)
+    finish(5)
+    finish(6)
     w_wait(2)
     wsums[0] = wsum[...]
     terms = [wsums[lax.rem(NREP + me_r - r, NREP)] for r in range(NREP)]
     wtotal[...] = (terms[0] + terms[1]) + (terms[2] + terms[3])
-    wrows[me_p * NZ + me_z] = wtotal[...]
-    w_start(3)
-    finish(5)
-    finish(6)
-    finish(7)
+    finish(7, True)
     own = pltpu.make_async_copy(sums.at[me_d], back.at[me_d], own_sem.at[0])
     own.start()
-    w_wait(3)
-    w_start(4)
     own.wait()
-    others(lambda n: came(n).wait_recv())
-    w_wait(4)
-    others(lambda n: to(n).wait_send())
-    for stage in range(5):
+    others(lambda i, k: came(i, k).wait_recv())
+    local_save.wait()
+    others(lambda i, k: to(i, k).wait_send())
+    for stage in range(3):
         for k in range(1, peers[stage]):
             w_stage(stage, k).wait_send()
 
@@ -505,10 +577,10 @@
         out_shape=(
             jax.ShapeDtypeStruct((NDOM, Q, FEAT), BF16),
             jax.ShapeDtypeStruct((LOCAL, TILE, FEAT), BF16),
-            jax.ShapeDtypeStruct((NDOM, WROWS, TILE), F32),
+            jax.ShapeDtypeStruct((WROWS, TILE), F32),
         ),
         in_specs=[ANY, VMEM],
-        out_specs=(VMEM, VMEM, VMEM),
+        out_specs=(VMEM, ANY, VMEM),
         scratch_shapes=[
             pltpu.VMEM((SRC, FEAT, TILE), BF16),
             pltpu.VMEM((NREP, NDOM, Q, FEAT), BF16),
@@ -519,17 +591,18 @@
             pltpu.VMEM((NZ, WROWS, TILE), F32),
             pltpu.VMEM((WROWS, TILE), F32),
             pltpu.VMEM((NREP, WROWS, TILE), F32),
-            pltpu.VMEM((WROWS, TILE), F32),
+            pltpu.VMEM((LOCAL, TILE, FEAT), BF16),
             dma((2,)),
-            dma((1,)),
+            dma((2,)),
             dma((NZ, NREP)),
             dma((NZ, NREP)),
             dma((NDOM,)),
             dma((NDOM,)),
-            dma((5, PLANE)),
-            dma((5, PLANE)),
+            dma((3, PLANE)),
+            dma((3, PLANE)),
         ],
-        compiler_params=pltpu.CompilerParams(collective_id=1, has_side_effects=True),
+        compiler_params=pltpu.CompilerParams(collective_id=1, has_side_effects=True, vmem_limit_bytes=14 << 20),
+        cost_estimate=busy(24),
         name="return_halo",
     )(sgt, wpart)
 
@@ -551,18 +624,22 @@
         loads[i].wait()
         wide[pl.ds(i * size, size), :] = raw[pl.ds(i * size, size), :].astype(F32)
 
-    @pl.loop(0, NDOM // LISTS)
-    def _(g):
-        for u in range(LISTS):
-            d = g * LISTS + u
-            live = counts[0, d]
-            places = []
-            for c in range(Q):
-                slot = rep * Q + c
-                places.append(jnp.where(slot < live, rows[0, d, slot], ROWS + c))
-            olds = [wide[pl.ds(row, 1), :] for row in places]
-            for c, row in enumerate(places):
-                wide[pl.ds(row, 1), :] = olds[c] + news[pl.ds(d * Q + c, 1), :]
+    for r in range(NREP):
+
+        @pl.when(rep == r)
+        def _():
+            @pl.loop(0, NDOM // LISTS)
+            def _(g):
+                for u in range(LISTS):
+                    d = g * LISTS + u
+                    live = counts[0, d]
+                    places = []
+                    for c in range(Q):
+                        row = rows[0, d, r * Q + c]
+                        places.append(jnp.where(r * Q + c < live, row, ROWS + c))
+                    olds = [wide[pl.ds(row, 1), :] for row in places]
+                    for c, row in enumerate(places):
+                        wide[pl.ds(row, 1), :] = olds[c] + news[pl.ds(d * Q + c, 1), :]
 
     saves = []
     for i in range(PIECES):
@@ -588,15 +665,21 @@
             pltpu.SemaphoreType.DMA((PIECES,)),
             pltpu.SemaphoreType.DMA((PIECES,)),
         ],
+        compiler_params=pltpu.CompilerParams(vmem_limit_bytes=14 << 20),
+        cost_estimate=busy(4),
         name="scatter_rows",
     )(rows, counts, local, back)
 
 
 def final_kernel(
-    part, inbox, held, mid, relayed, load_sem, ring_send, ring_recv,
+    part, wtotal, inbox, wrows,
+    held, mid, relayed, load_sem, own_sem, ring_send, ring_recv, w_send, w_recv,
 ):
     me_d, me_r, right, across, left = place()
     greet([(me_d, right), (me_d, left)])
+    me_z, me_p = me_d // PLANE, lax.rem(me_d, PLANE)
+    greet([(lax.rem(me_z + k, NZ) * PLANE + me_p, me_r) for k in range(1, NZ)])
+    greet([(me_z * PLANE + lax.rem(me_p + k, PLANE), me_r) for k in range(1, PLANE)])
     loads = [
         pltpu.make_async_copy(part.at[r], held.at[r], load_sem.at[i])
         for i, r in enumerate((across, right, left))
@@ -628,43 +711,82 @@
         ring(i, 4).start()
         ring(i, 5).start()
 
+    def w_line(k, came):
+        z = lax.rem(me_z + k, NZ)
+        y = lax.rem(me_z + NZ - k, NZ) if came else me_z
+        return remote(
+            wtotal, wrows.at[me_p * NZ + y], w_send.at[0, k], w_recv.at[0, k],
+            (z * PLANE + me_p, me_r),
+        )
+
+    def w_plane(k, came):
+        p = lax.rem(me_p + k, PLANE)
+        q = lax.rem(me_p + PLANE - k, PLANE) if came else me_p
+        return remote(
+            wrows.at[pl.ds(me_p * NZ, NZ)], wrows.at[pl.ds(q * NZ, NZ)],
+            w_send.at[1, k], w_recv.at[1, k], (me_z * PLANE + p, me_r),
+        )
+
     for load in loads:
         load.wait()
-    greeted(2)
+    greeted(2 + NZ - 1 + PLANE - 1)
     for j in range(4):
         ring(0, j).start()
+    for k in range(1, NZ):
+        w_line(k, False).start()
+    own = pltpu.make_async_copy(wtotal, wrows.at[me_p * NZ + me_z], own_sem)
+    own.start()
     for i in range(PARTS):
         if i + 1 < PARTS:
             for j in range(4):
                 ring(i + 1, j).start()
         relay(i)
+        if i == PARTS // 2:
+            own.wait()
+            for k in range(1, NZ):
+                w_line(k, True).wait_recv()
+            for k in range(1, PLANE):
+                w_plane(k, False).start()
+    for k in range(1, PLANE):
+        w_plane(k, True).wait_recv()
     for i in range(PARTS):
         for j in range(2, 6):
             ring(i, j).wait_recv()
+    for k in range(1, NZ):
+        w_line(k, False).wait_send()
+    for k in range(1, PLANE):
+        w_plane(k, False).wait_send()
     for i in range(PARTS):
         for j in range(6):
             ring(i, j).wait_send()
 
 
-def final_sums(part):
+def final_sums(part, wtotal):
     rows = ROWS // NREP
     dma = pltpu.SemaphoreType.DMA
     return pl.pallas_call(
         final_kernel,
-        out_shape=jax.ShapeDtypeStruct((2, rows, FEAT), BF16),
-        in_specs=[ANY],
-        out_specs=VMEM,
+        out_shape=(
+            jax.ShapeDtypeStruct((2, rows, FEAT), BF16),
+            jax.ShapeDtypeStruct((NDOM, WROWS, TILE), F32),
+        ),
+        in_specs=[ANY, VMEM],
+        out_specs=(VMEM, VMEM),
         scratch_shapes=[
             pltpu.VMEM((NREP, rows, FEAT), BF16),
             pltpu.VMEM((2, PARTS, rows // PARTS // 2, FEAT), BF16),
             pltpu.VMEM((2, PARTS, rows // PARTS // 2, FEAT), BF16),
             dma((3,)),
+            dma,
             dma((PARTS, 6)),
             dma((PARTS, 6)),
+            dma((2, PLANE)),
+            dma((2, PLANE)),
         ],
-        compiler_params=pltpu.CompilerParams(collective_id=2, has_side_effects=True),
+        compiler_params=pltpu.CompilerParams(collective_id=2, has_side_effects=True, vmem_limit_bytes=8 << 20),
+        cost_estimate=busy(20),
         name="final_sums",
-    )(part)
+    )(part, wtotal)
 
 
 def shards(
@@ -680,10 +802,10 @@
         out_grad,
         weight,
     )
-    back, local, wrows = return_halo(sgt, wpart.reshape(NDOM, WROWS, TILE))
+    back, local, wtotal = return_halo(sgt, wpart.reshape(NDOM, WROWS, TILE))
     node_part = scatter_rows(send_rows, send_count, local.reshape(ROWS, FEAT), back)
     node_part = node_part.reshape(NREP, ROWS // NREP, FEAT)
-    sums = final_sums(node_part)
+    sums, wrows = final_sums(node_part, wtotal)
     own = lax.dynamic_index_in_dim(node_part, lax.axis_index("rep"), 0, keepdims=False)
     node_grad = (own.astype(F32) + sums[0].astype(F32) + sums[1].astype(F32)).astype(BF16)
     weight_grad = wrows.reshape(2, FEAT, TILE).transpose(1, 0, 2).reshape(FEAT, 2 * TILE)

time: 122 us -> 104 us (0.85)
  Pallas kernels: 118 us -> 98.1 us
  local copies, waits for them, and re-layouts: 0.67 us -> 3.7 us
  other arithmetic: 2.36 us -> 1 us
    pallas_call x1, Pallas kernels: 33.2 us -> 26 us  [return_halo(): pl.pallas_call(return_kernel, out_shape=(jax.ShapeDtypeStruct((NDOM, Q, F...]
    pallas_call x1, Pallas kernels: 21.3 us -> 16.2 us  [layer(): pl.pallas_call(layer_kernel, out_shape=(jax.ShapeDtypeStruct((TGT * TILE,...]
    pallas_call x1, Pallas kernels: 7.83 us -> 3.94 us  [scatter_rows(): pl.pallas_call(scatter_kernel, out_shape=jax.ShapeDtypeStruct((ROWS, FEAT...]
    pallas_call x1, Pallas kernels: 33.7 us -> 30 us  [exchange_halo(): pl.pallas_call(halo_kernel, out_shape=jax.ShapeDtypeStruct((NREP, NDOM, Q...]
    unnamed x2 -> x22, local copies, waits for them, and re-layouts: 0.01 us -> 3.03 us
    convert_element_type x1, other arithmetic: 2.36 us -> 1 us  [shards(): (own.astype(F32) + sums[0].astype(F32) + sums[1].astype(F32)).astype(BF16)]
where the time goes in v3:
time: 104 us
  Pallas kernels  98.1 us (94%)
  local copies, waits for them, and re-layouts  3.7 us (4%)
    pallas_call x1, Pallas kernels, exchange_halo(): pl.pallas_call(halo_kernel, out_shape=jax.ShapeDtypeStruct((NREP, NDOM, Q...  30 us
    pallas_call x1, Pallas kernels, return_halo(): pl.pallas_call(return_kernel, out_shape=(jax.ShapeDtypeStruct((NDOM, Q, F...  26 us
    pallas_call x1, Pallas kernels, final_sums(): pl.pallas_call(final_kernel, out_shape=(jax.ShapeDtypeStruct((2, rows, FE...  21.9 us
    pallas_call x1, Pallas kernels, layer(): pl.pallas_call(layer_kernel, out_shape=(jax.ShapeDtypeStruct((TGT * TILE,...  16.2 us
    pallas_call x1, Pallas kernels, scatter_rows(): pl.pallas_call(scatter_kernel, out_shape=jax.ShapeDtypeStruct((ROWS, FEAT...  3.94 us
    unnamed x22, local copies, waits for them, and re-layouts  3.03 us

profile of v3, /device:TPU:1, one launch (start us, length us, event | category | flops | bytes accessed | tf_op | source)
XLA Modules:
  0.0 103.6 jit_solution(9094277248712012370)
XLA Ops:
  0.6 0.0 copy-start.1
  0.6 1.6 %copy-done.1 = bf16[8192,128]{1,0:T(8,128)(2,1)S(1)} copy-done((bf16[8192,128]{1,0:T(8,128)(2,1)S(1)}, bf16[8192,128]{1,0:T(8,128)(2,1)}, u32[]{:S(2)}) %copy-start.1) | copy-done | bytes 2097176
  2.2 0.0 copy-start.5
  2.2 0.8 copy-done.5
  3.0 0.0 copy-start.9
  3.0 0.7 copy-done.9
  3.6 0.0 copy-start
  3.6 0.0 copy-start.2
  3.6 0.0 copy-start.3
  3.6 0.0 copy-start.4
  3.6 0.0 copy-start.7
  3.7 0.0 copy-start.8
  3.7 30.0 %exchange_halo.1.halo = bf16[4,64,16,128]{3,2,1,0:T(8,128)(2,1)S(1)} custom-call(s32[1,64,64]{2,1,0:T(8,128)S(1)} %copy-done.5, s32[1,64]{1,0:T(1,128)S(1)} %copy-done.9, bf16[8192,128]{1,0:T(8,128)(2,1)S(1)} %copy-done.1), custom_call_target="tpu_custom_call" | custom-call | flops 9600000000 | bytes 72000000 | tf_op jit(solution)/shard_map/exchange_halo/pallas_call | solution.py:256
  33.7 0.0 copy-done
  33.7 0.0 copy-done.2
  33.7 0.0 copy-done.3
  33.7 0.0 copy-done.4
  33.7 0.0 copy-done.7
  33.7 0.0 copy-done.8
  33.7 16.2 %layer.1 = (bf16[2048,256]{1,0:T(8,128)(2,1)}, bf16[96,128,128]{2,1,0:T(8,128)(2,1)S(1)}, f32[256,128]{1,0:T(8,128)S(1)}) custom-call(s32[1,1,256]{2,1,0:T(1,128)S(1)} %copy-done.7, s32[1,1,256]{2,1,0:T(1,128)S(1)} %copy-done.8, bf16[128,4,16,128]{3,2,1,0:T(8,128)(2,1)S(1)} %bitcast.18, bf16[4,64,16,128]{3,2,1,0:T(8,128)(2,1)S(1)} %exchange_halo.1.halo, ...), custom_call_target="tpu_custom_call" | custom-call | flops 6400000000 | bytes 48000000 | tf_op jit(solution)/shard_map/layer/pallas_call | solution.py:375
  49.9 0.0 copy-start.6
  49.9 0.0 copy-start.10
  50.0 26.0 %return_halo.1 = (bf16[64,16,128]{2,1,0:T(8,128)(2,1)S(1)}, bf16[64,128,128]{2,1,0:T(8,128)(2,1)S(1)}, f32[4,128]{1,0:T(4,128)S(1)}) custom-call(bf16[96,128,128]{2,1,0:T(8,128)(2,1)S(1)} %get-tuple-element.12.sgt, f32[64,4,128]{2,1,0:T(4,128)S(1)} %bitcast.20), custom_call_target="tpu_custom_call" | custom-call | flops 9600000000 | bytes 72000000 | tf_op jit(solution)/shard_map/return_halo/pallas_call | solution.py:575
  76.0 0.0 copy-done.6
  76.0 0.0 copy-done.10
  76.0 3.9 %scatter_rows.1 = bf16[8192,128]{1,0:T(8,128)(2,1)S(1)} custom-call(s32[1,64,64]{2,1,0:T(8,128)S(1)} %copy-done.6, s32[1,64]{1,0:T(1,128)S(1)} %copy-done.10, bf16[8192,128]{1,0:T(8,128)(2,1)S(1)} %bitcast.19, bf16[64,16,128]{2,1,0:T(8,128)(2,1)S(1)} %get-tuple-element.15.back), custom_call_target="tpu_custom_call" | custom-call | flops 1600000000 | bytes 12000000 | tf_op jit(solution)/shard_map/scatter_rows/pallas_call | solution.py:655
  80.0 21.9 %final_sums.1 = (bf16[2,2048,128]{2,1,0:T(8,128)(2,1)S(1)}, f32[64,4,128]{2,1,0:T(4,128)S(1)}) custom-call(bf16[4,2048,128]{2,1,0:T(8,128)(2,1)S(1)} %bitcast.14, f32[4,128]{1,0:T(4,128)S(1)} %get-tuple-element.16.wtotal), custom_call_target="tpu_custom_call" | custom-call | flops 8000000000 | bytes 60000000 | tf_op jit(solution)/shard_map/final_sums/pallas_call | solution.py:767
  101.9 1.0 fusion
  102.9 0.7 copy.14
Async XLA Ops:
  0.6 1.6 %copy-start.1 = (bf16[8192,128]{1,0:T(8,128)(2,1)S(1)}, bf16[8192,128]{1,0:T(8,128)(2,1)}, u32[]{:S(2)}) copy-start(bf16[8192,128]{1,0:T(8,128)(2,1)} %feats.1) | copy-start | bytes 6291460
  2.2 0.8 copy-start.5
  3.0 0.7 copy-start.9
  3.6 30.0 %copy-start = (bf16[1,1,256,128,128]{4,3,2,1,0:T(8,128)(2,1)S(1)}, bf16[1,1,256,128,128]{4,3,2,1,0:T(8,128)(2,1)}, u32[]{:S(2)}) copy-start(bf16[1,1,256,128,128]{4,3,2,1,0:T(8,128)(2,1)} %param.15) | copy-start | bytes 25165828
  3.6 30.0 %copy-start.2 = (bf16[8192,128]{1,0:T(8,128)(2,1)S(1)}, bf16[8192,128]{1,0:T(8,128)(2,1)}, u32[]{:S(2)}) copy-start(bf16[8192,128]{1,0:T(8,128)(2,1)} %feats.1) | copy-start | bytes 6291460
  3.6 30.0 %copy-start.3 = (bf16[2048,256]{1,0:T(8,128)(2,1)S(1)}, bf16[2048,256]{1,0:T(8,128)(2,1)}, u32[]{:S(2)}) copy-start(bf16[2048,256]{1,0:T(8,128)(2,1)} %grads.1) | copy-start | bytes 3145732
  3.6 30.0 %copy-start.4 = (bf16[128,256]{1,0:T(8,128)(2,1)S(1)}, bf16[128,256]{1,0:T(8,128)(2,1)}, u32[]{:S(2)}) copy-start(bf16[128,256]{1,0:T(8,128)(2,1)} %weight.1) | copy-start | bytes 196612
  3.6 30.0 %copy-start.7 = (s32[1,1,256]{2,1,0:T(1,128)S(1)}, s32[1,1,256]{2,1,0:T(1,128)}, u32[]{:S(2)}) copy-start(s32[1,1,256]{2,1,0:T(1,128)} %targets.1) | copy-start | bytes 3076
  3.7 30.0 %copy-start.8 = (s32[1,1,256]{2,1,0:T(1,128)S(1)}, s32[1,1,256]{2,1,0:T(1,128)}, u32[]{:S(2)}) copy-start(s32[1,1,256]{2,1,0:T(1,128)} %anchors.1) | copy-start | bytes 3076
  49.9 26.1 %copy-start.6 = (s32[1,64,64]{2,1,0:T(8,128)S(1)}, s32[1,64,64]{2,1,0:T(8,128)}, u32[]{:S(2)}) copy-start(s32[1,64,64]{2,1,0:T(8,128)} %rows.1) | copy-start | bytes 49156
  49.9 26.1 %copy-start.10 = (s32[1,64]{1,0:T(1,128)S(1)}, s32[1,64]{1,0:T(1,128)}, u32[]{:S(2)}) copy-start(s32[1,64]{1,0:T(1,128)} %counts.1) | copy-start | bytes 772

commit v4 on v3

--- a/solution.py
+++ b/solution.py
@@ -45,7 +45,6 @@
 DENSE = 8
 SAVES = 3
 LISTS = 2
-PIECES = 4
 LAG = 3
 RELAYED = 6
 WROWS = 2 * FEAT // NDOM
@@ -280,10 +279,9 @@
 
 
 def layer_kernel(
-    targets, anchors, feats, halo, tiles, grads, weight,
+    targets, anchors, feats, halo, wt, og, weight,
     act_out, sgt_out, wgrad_out,
-    src, wt, og, agg, gt, sg, act, sgb, wg,
-    src_sem, wt_sem, og_sem, out_sem,
+    src, agg, gt, sg, act, sgb, wg, src_sem, out_sem,
 ):
     loads = [
         pltpu.make_async_copy(feats, src.at[pl.ds(0, 2 * LOCAL)], src_sem.at[NREP])
@@ -294,15 +292,6 @@
     for load in loads:
         load.start()
 
-    def tile_load(c):
-        part = pl.ds(c * PER, PER)
-        return pltpu.make_async_copy(tiles.at[part], wt.at[part], wt_sem.at[c])
-
-    for c in range(CHUNKS):
-        tile_load(c).start()
-    grad_load = pltpu.make_async_copy(grads, og, og_sem)
-    grad_load.start()
-
     agg[...] = jnp.zeros_like(agg)
     sg[...] = jnp.zeros_like(sg)
     wg[...] = jnp.zeros_like(wg)
@@ -311,15 +300,12 @@
 
     @pl.loop(0, CHUNKS)
     def _(c):
-        tile_load(c).wait()
         for u in range(PER):
             t = c * PER + u
             block = src[pl.ds(anchors[0, 0, t] * 2, 2)].reshape(TILE, FEAT)
             prod = jnp.dot(wt[t], block, preferred_element_type=F32)
             k = targets[0, 0, t]
             agg[k] = agg[k] + prod
-
-    grad_load.wait()
 
     @pl.loop(0, TGT // DENSE)
     def _(c):
@@ -379,12 +365,10 @@
             jax.ShapeDtypeStruct((SRC, FEAT, TILE), BF16),
             jax.ShapeDtypeStruct((2 * FEAT, TILE), F32),
         ),
-        in_specs=[SMEM, SMEM, ANY, ANY, ANY, ANY, VMEM],
+        in_specs=[SMEM, SMEM, ANY, ANY, VMEM, VMEM, VMEM],
         out_specs=(ANY, ANY, VMEM),
         scratch_shapes=[
             pltpu.VMEM((2 * SRC, NREP, Q, FEAT), BF16),
-            pltpu.VMEM((NT, TILE, TILE), BF16),
-            pltpu.VMEM((TGT * TILE, HID), BF16),
             pltpu.VMEM((TGT, TILE, FEAT), F32),
             pltpu.VMEM((TGT, FEAT, TILE), BF16),
             pltpu.VMEM((SRC, FEAT, TILE), F32),
@@ -392,8 +376,6 @@
             pltpu.VMEM((SRC, FEAT, TILE), BF16),
             pltpu.VMEM((FEAT, HID), F32),
             pltpu.SemaphoreType.DMA((NREP + 1,)),
-            pltpu.SemaphoreType.DMA((CHUNKS,)),
-            pltpu.SemaphoreType.DMA,
             pltpu.SemaphoreType.DMA((1 + SAVES,)),
         ],
         compiler_params=pltpu.CompilerParams(vmem_limit_bytes=30 << 20),
@@ -403,22 +385,14 @@
 
 
 def return_kernel(
-    sgt, wpart, back, local, wtotal,
-    turned, part, inbox, sums, wbox, wplane, wline, wsum, wsums, upright_local,
-    load_sem, own_sem, ring_send, ring_recv, send_sem, recv_sem, w_send, w_recv,
+    turned, wpart, back, local, wtotal,
+    part, inbox, sums, wbox, wplane, wline, wsum, wsums, upright_local,
+    own_sem, ring_send, ring_recv, send_sem, recv_sem, w_send, w_recv,
 ):
     me_d, me_r, right, across, left = place()
     greet_dom(me_d, me_r)
     greet([(me_d, right), (me_d, left), (me_d, across)])
 
-    halo_load = pltpu.make_async_copy(
-        sgt.at[pl.ds(LOCAL, SRC - LOCAL)], turned.at[pl.ds(LOCAL, SRC - LOCAL)], load_sem.at[0]
-    )
-    local_load = pltpu.make_async_copy(
-        sgt.at[pl.ds(0, LOCAL)], turned.at[pl.ds(0, LOCAL)], load_sem.at[1]
-    )
-    halo_load.start()
-    local_load.start()
     one = (
         lax.broadcasted_iota(jnp.int32, (TILE, TILE), 0)
         == lax.broadcasted_iota(jnp.int32, (TILE, TILE), 1)
@@ -428,8 +402,6 @@
         return lax.dot_general(
             one, block, (((1,), (1,)), ((), ())), preferred_element_type=F32
         ).astype(BF16)
-
-    halo_load.wait()
 
     @pl.loop(0, (SRC - LOCAL) // 8)
     def _(c):
@@ -511,7 +483,6 @@
             ring(i, k).start()
 
     w_start(0)
-    local_load.wait()
 
     @pl.loop(0, LOCAL // 8)
     def _(i):
@@ -579,10 +550,9 @@
             jax.ShapeDtypeStruct((LOCAL, TILE, FEAT), BF16),
             jax.ShapeDtypeStruct((WROWS, TILE), F32),
         ),
-        in_specs=[ANY, VMEM],
+        in_specs=[VMEM, VMEM],
         out_specs=(VMEM, ANY, VMEM),
         scratch_shapes=[
-            pltpu.VMEM((SRC, FEAT, TILE), BF16),
             pltpu.VMEM((NREP, NDOM, Q, FEAT), BF16),
             pltpu.VMEM((NREP, NDOM, Q, FEAT), BF16),
             pltpu.VMEM((NDOM, Q, FEAT), BF16),
@@ -592,7 +562,6 @@
             pltpu.VMEM((WROWS, TILE), F32),
             pltpu.VMEM((NREP, WROWS, TILE), F32),
             pltpu.VMEM((LOCAL, TILE, FEAT), BF16),
-            dma((2,)),
             dma((2,)),
             dma((NZ, NREP)),
             dma((NZ, NREP)),
@@ -607,22 +576,11 @@
     )(sgt, wpart)
 
 
-def scatter_kernel(rows, counts, local, back, out, raw, wide, news, done, in_sem, out_sem):
+def scatter_kernel(rows, counts, local, back, out, wide, news):
     rep = lax.axis_index("rep")
-    size = ROWS // PIECES
-    loads = [
-        pltpu.make_async_copy(
-            local.at[pl.ds(i * size, size)], raw.at[pl.ds(i * size, size)], in_sem.at[i]
-        )
-        for i in range(PIECES)
-    ]
-    for load in loads:
-        load.start()
     wide[pl.ds(ROWS, Q), :] = jnp.zeros((Q, FEAT), F32)
     news[...] = back[...].reshape(NDOM * Q, FEAT).astype(F32)
-    for i in range(PIECES):
-        loads[i].wait()
-        wide[pl.ds(i * size, size), :] = raw[pl.ds(i * size, size), :].astype(F32)
+    wide[pl.ds(0, ROWS), :] = local[...].astype(F32)
 
     for r in range(NREP):
 
@@ -641,29 +599,18 @@
                     for c, row in enumerate(places):
                         wide[pl.ds(row, 1), :] = olds[c] + news[pl.ds(d * Q + c, 1), :]
 
-    saves = []
-    for i in range(PIECES):
-        part = pl.ds(i * size, size)
-        done[part, :] = wide[part, :].astype(BF16)
-        saves.append(pltpu.make_async_copy(done.at[part], out.at[part], out_sem.at[i]))
-        saves[-1].start()
-    for save in saves:
-        save.wait()
+    out[...] = wide[pl.ds(0, ROWS), :].astype(BF16)
 
 
 def scatter_rows(rows, counts, local, back):
     return pl.pallas_call(
         scatter_kernel,
         out_shape=jax.ShapeDtypeStruct((ROWS, FEAT), BF16),
-        in_specs=[SMEM, SMEM, ANY, VMEM],
-        out_specs=ANY,
+        in_specs=[SMEM, SMEM, VMEM, VMEM],
+        out_specs=VMEM,
         scratch_shapes=[
-            pltpu.VMEM((ROWS, FEAT), BF16),
             pltpu.VMEM((ROWS + Q, FEAT), F32),
             pltpu.VMEM((NDOM * Q, FEAT), F32),
-            pltpu.VMEM((ROWS, FEAT), BF16),
-            pltpu.SemaphoreType.DMA((PIECES,)),
-            pltpu.SemaphoreType.DMA((PIECES,)),
         ],
         compiler_params=pltpu.CompilerParams(vmem_limit_bytes=14 << 20),
         cost_estimate=busy(4),
@@ -672,20 +619,14 @@
 
 
 def final_kernel(
-    part, wtotal, inbox, wrows,
-    held, mid, relayed, load_sem, own_sem, ring_send, ring_recv, w_send, w_recv,
+    held, wtotal, inbox, wrows,
+    mid, relayed, own_sem, ring_send, ring_recv, w_send, w_recv,
 ):
     me_d, me_r, right, across, left = place()
     greet([(me_d, right), (me_d, left)])
     me_z, me_p = me_d // PLANE, lax.rem(me_d, PLANE)
     greet([(lax.rem(me_z + k, NZ) * PLANE + me_p, me_r) for k in range(1, NZ)])
     greet([(me_z * PLANE + lax.rem(me_p + k, PLANE), me_r) for k in range(1, PLANE)])
-    loads = [
-        pltpu.make_async_copy(part.at[r], held.at[r], load_sem.at[i])
-        for i, r in enumerate((across, right, left))
-    ]
-    for load in loads:
-        load.start()
     size = ROWS // NREP // PARTS // 2
 
     def ring(i, j):
@@ -727,8 +668,6 @@
             w_send.at[1, k], w_recv.at[1, k], (me_z * PLANE + p, me_r),
         )
 
-    for load in loads:
-        load.wait()
     greeted(2 + NZ - 1 + PLANE - 1)
     for j in range(4):
         ring(0, j).start()
@@ -770,13 +709,11 @@
             jax.ShapeDtypeStruct((2, rows, FEAT), BF16),
             jax.ShapeDtypeStruct((NDOM, WROWS, TILE), F32),
         ),
-        in_specs=[ANY, VMEM],
+        in_specs=[VMEM, VMEM],
         out_specs=(VMEM, VMEM),
         scratch_shapes=[
-            pltpu.VMEM((NREP, rows, FEAT), BF16),
             pltpu.VMEM((2, PARTS, rows // PARTS // 2, FEAT), BF16),
             pltpu.VMEM((2, PARTS, rows // PARTS // 2, FEAT), BF16),
-            dma((3,)),
             dma,
             dma((PARTS, 6)),
             dma((PARTS, 6)),

time: 104 us -> 103 us (level)
  no operation moved by 1% of the time
where the time goes in v4:
time: 103 us
  Pallas kernels  97.3 us (94%)
  local copies, waits for them, and re-layouts  3.7 us (4%)
    pallas_call x1, Pallas kernels, exchange_halo(): pl.pallas_call(halo_kernel, out_shape=jax.ShapeDtypeStruct((NREP, NDOM, Q...  30 us
    pallas_call x1, Pallas kernels, return_halo(): pl.pallas_call(return_kernel, out_shape=(jax.ShapeDtypeStruct((NDOM, Q, F...  26 us
    pallas_call x1, Pallas kernels, final_sums(): pl.pallas_call(final_kernel, out_shape=(jax.ShapeDtypeStruct((2, rows, FE...  21.8 us
    pallas_call x1, Pallas kernels, layer(): pl.pallas_call(layer_kernel, out_shape=(jax.ShapeDtypeStruct((TGT * TILE,...  15.9 us
    pallas_call x1, Pallas kernels, scatter_rows(): pl.pallas_call(scatter_kernel, out_shape=jax.ShapeDtypeStruct((ROWS, FEAT...  3.54 us
    unnamed x22, local copies, waits for them, and re-layouts  3.03 us

profile of v4, /device:TPU:1, one launch (start us, length us, event | category | flops | bytes accessed | tf_op | source)
XLA Modules:
  0.0 102.8 jit_solution(17119822214798908310)
XLA Ops:
  0.6 0.0 copy-start.1
  0.6 1.6 %copy-done.1 = bf16[8192,128]{1,0:T(8,128)(2,1)S(1)} copy-done((bf16[8192,128]{1,0:T(8,128)(2,1)S(1)}, bf16[8192,128]{1,0:T(8,128)(2,1)}, u32[]{:S(2)}) %copy-start.1) | copy-done | bytes 2097176
  2.2 0.0 copy-start.5
  2.2 0.8 copy-done.5
  3.0 0.0 copy-start.9
  3.0 0.7 copy-done.9
  3.6 0.0 copy-start
  3.6 0.0 copy-start.2
  3.6 0.0 copy-start.3
  3.6 0.0 copy-start.4
  3.6 0.0 copy-start.7
  3.7 0.0 copy-start.8
  3.7 30.0 %exchange_halo.1.halo = bf16[4,64,16,128]{3,2,1,0:T(8,128)(2,1)S(1)} custom-call(s32[1,64,64]{2,1,0:T(8,128)S(1)} %copy-done.5, s32[1,64]{1,0:T(1,128)S(1)} %copy-done.9, bf16[8192,128]{1,0:T(8,128)(2,1)S(1)} %copy-done.1), custom_call_target="tpu_custom_call" | custom-call | flops 9600000000 | bytes 72000000 | tf_op jit(solution)/shard_map/exchange_halo/pallas_call | solution.py:255
  33.7 0.0 copy-done
  33.7 0.0 copy-done.2
  33.7 0.0 copy-done.3
  33.7 0.0 copy-done.4
  33.7 0.0 copy-done.7
  33.7 0.0 copy-done.8
  33.7 15.9 %layer.1 = (bf16[2048,256]{1,0:T(8,128)(2,1)}, bf16[96,128,128]{2,1,0:T(8,128)(2,1)S(1)}, f32[256,128]{1,0:T(8,128)S(1)}) custom-call(s32[1,1,256]{2,1,0:T(1,128)S(1)} %copy-done.7, s32[1,1,256]{2,1,0:T(1,128)S(1)} %copy-done.8, bf16[128,4,16,128]{3,2,1,0:T(8,128)(2,1)S(1)} %bitcast.18, bf16[4,64,16,128]{3,2,1,0:T(8,128)(2,1)S(1)} %exchange_halo.1.halo, ...), custom_call_target="tpu_custom_call" | custom-call | flops 6400000000 | bytes 48000000 | tf_op jit(solution)/shard_map/layer/pallas_call | solution.py:361
  49.6 0.0 copy-start.6
  49.7 0.0 copy-start.10
  49.7 26.0 %return_halo.1 = (bf16[64,16,128]{2,1,0:T(8,128)(2,1)S(1)}, bf16[64,128,128]{2,1,0:T(8,128)(2,1)S(1)}, f32[4,128]{1,0:T(4,128)S(1)}) custom-call(bf16[96,128,128]{2,1,0:T(8,128)(2,1)S(1)} %get-tuple-element.12.turned, f32[64,4,128]{2,1,0:T(4,128)S(1)} %bitcast.20), custom_call_target="tpu_custom_call" | custom-call | flops 9600000000 | bytes 72000000 | tf_op jit(solution)/shard_map/return_halo/pallas_call | solution.py:546
  75.7 0.0 copy-done.6
  75.7 0.0 copy-done.10
  75.7 3.5 %scatter_rows.1 = bf16[8192,128]{1,0:T(8,128)(2,1)S(1)} custom-call(s32[1,64,64]{2,1,0:T(8,128)S(1)} %copy-done.6, s32[1,64]{1,0:T(1,128)S(1)} %copy-done.10, bf16[8192,128]{1,0:T(8,128)(2,1)S(1)} %bitcast.19, bf16[64,16,128]{2,1,0:T(8,128)(2,1)S(1)} %get-tuple-element.15.back), custom_call_target="tpu_custom_call" | custom-call | flops 1600000000 | bytes 12000000 | tf_op jit(solution)/shard_map/scatter_rows/pallas_call | solution.py:606
  79.3 21.8 %final_sums.1 = (bf16[2,2048,128]{2,1,0:T(8,128)(2,1)S(1)}, f32[64,4,128]{2,1,0:T(4,128)S(1)}) custom-call(bf16[4,2048,128]{2,1,0:T(8,128)(2,1)S(1)} %bitcast.14, f32[4,128]{1,0:T(4,128)S(1)} %get-tuple-element.16.wtotal), custom_call_target="tpu_custom_call" | custom-call | flops 8000000000 | bytes 60000000 | tf_op jit(solution)/shard_map/final_sums/pallas_call | solution.py:706
  101.1 1.0 fusion
  102.1 0.7 copy.14
Async XLA Ops:
  0.6 1.6 %copy-start.1 = (bf16[8192,128]{1,0:T(8,128)(2,1)S(1)}, bf16[8192,128]{1,0:T(8,128)(2,1)}, u32[]{:S(2)}) copy-start(bf16[8192,128]{1,0:T(8,128)(2,1)} %feats.1) | copy-start | bytes 6291460
  2.2 0.8 copy-start.5
  3.0 0.7 copy-start.9
  3.6 30.0 %copy-start = (bf16[1,1,256,128,128]{4,3,2,1,0:T(8,128)(2,1)S(1)}, bf16[1,1,256,128,128]{4,3,2,1,0:T(8,128)(2,1)}, u32[]{:S(2)}) copy-start(bf16[1,1,256,128,128]{4,3,2,1,0:T(8,128)(2,1)} %param.15) | copy-start | bytes 25165828
  3.6 30.0 %copy-start.2 = (bf16[8192,128]{1,0:T(8,128)(2,1)S(1)}, bf16[8192,128]{1,0:T(8,128)(2,1)}, u32[]{:S(2)}) copy-start(bf16[8192,128]{1,0:T(8,128)(2,1)} %feats.1) | copy-start | bytes 6291460
  3.6 30.0 %copy-start.3 = (bf16[2048,256]{1,0:T(8,128)(2,1)S(1)}, bf16[2048,256]{1,0:T(8,128)(2,1)}, u32[]{:S(2)}) copy-start(bf16[2048,256]{1,0:T(8,128)(2,1)} %og.1) | copy-start | bytes 3145732
  3.6 30.0 %copy-start.4 = (bf16[128,256]{1,0:T(8,128)(2,1)S(1)}, bf16[128,256]{1,0:T(8,128)(2,1)}, u32[]{:S(2)}) copy-start(bf16[128,256]{1,0:T(8,128)(2,1)} %weight.1) | copy-start | bytes 196612
  3.6 30.0 %copy-start.7 = (s32[1,1,256]{2,1,0:T(1,128)S(1)}, s32[1,1,256]{2,1,0:T(1,128)}, u32[]{:S(2)}) copy-start(s32[1,1,256]{2,1,0:T(1,128)} %targets.1) | copy-start | bytes 3076
  3.7 30.0 %copy-start.8 = (s32[1,1,256]{2,1,0:T(1,128)S(1)}, s32[1,1,256]{2,1,0:T(1,128)}, u32[]{:S(2)}) copy-start(s32[1,1,256]{2,1,0:T(1,128)} %anchors.1) | copy-start | bytes 3076
  49.6 26.1 %copy-start.6 = (s32[1,64,64]{2,1,0:T(8,128)S(1)}, s32[1,64,64]{2,1,0:T(8,128)}, u32[]{:S(2)}) copy-start(s32[1,64,64]{2,1,0:T(8,128)} %rows.1) | copy-start | bytes 49156
  49.7 26.1 %copy-start.10 = (s32[1,64]{1,0:T(1,128)S(1)}, s32[1,64]{1,0:T(1,128)}, u32[]{:S(2)}) copy-start(s32[1,64]{1,0:T(1,128)} %counts.1) | copy-start | bytes 772
